TPU v7x, 8 devices: a whole 2x2x1 slice. The times are simulated.
8 devices in a mesh: depth: 2 (over z, y), col: 2 (over x), row: 2 (over core).
Axes of the slice: x: 2, y: 2, z: 1, core: 2. Of those that a mesh axis runs over, the one named last changes fastest.
Arguments:
- tokens: bfloat16 [8192, 2048], P(('depth', 'row'), 'col')
- w_in: bfloat16 [2048, 16384], P('row', 'col')
- w_out: bfloat16 [16384, 2048], P('row', 'col')
- grad_y: bfloat16 [8192, 2048], P(('depth', 'row'), 'col')
Outputs:
- output 1: bfloat16 [8192, 2048], P(('depth', 'row'), 'col')
- output 2: bfloat16 [8192, 2048], P(('depth', 'row'), 'col')
- output 3: float32 [2048, 16384], P('row', 'col')
- output 4: float32 [16384, 2048], P('row', 'col')
All inputs are finite; a program needn't handle non-finite values.
Results may differ from a plain program's by a relative error of at most 0.00115.
Values are sent between devices in bfloat16 or wider.
A program may use at most 1 GiB of HBM per device.

v0:
```python
import jax
import jax.numpy as jnp
from jax import lax
from jax.sharding import PartitionSpec as P


def gelu_tanh(pre_act):
    return jax.nn.gelu(pre_act, approximate=True)


def contract_last(lhs, rhs):
    return lax.dot_general(lhs, rhs, (((1,), (1,)), ((), ())), preferred_element_type=jnp.float32)


def contract_first(lhs, rhs):
    return lax.dot_general(lhs, rhs, (((0,), (0,)), ((), ())), preferred_element_type=jnp.float32)


def gather_pre(tok_loc, w_in_loc):
    tok_full = lax.all_gather(tok_loc, "col", axis=1, tiled=True)
    w_in_cols = lax.all_gather(w_in_loc, "row", axis=0, tiled=True)
    pre_act = jnp.dot(tok_full, w_in_cols, preferred_element_type=jnp.float32)
    return tok_full, w_in_cols, pre_act


def solution(mesh):
    act_spec = P(("depth", "row"), "col")
    weight_spec = P("row", "col")

    def device_step(tok_loc, w_in_loc, w_out_loc, grad_loc):
        pre_act = gather_pre(tok_loc, w_in_loc)[2]
        hidden = gelu_tanh(pre_act).astype(jnp.bfloat16)
        hidden_full = lax.all_gather(hidden, "col", axis=1, tiled=True)
        w_out_cols = lax.all_gather(w_out_loc, "row", axis=0, tiled=True)
        y_loc = jnp.dot(hidden_full, w_out_cols, preferred_element_type=jnp.float32).astype(jnp.bfloat16)
        y_loc, tok_b, w_in_b, w_out_b, grad_b = lax.optimization_barrier((y_loc, tok_loc, w_in_loc, w_out_loc, grad_loc))
        tok_full, w_in_cols, pre_again = gather_pre(tok_b, w_in_b)
        hidden_again = gelu_tanh(pre_again).astype(jnp.bfloat16)
        w_out_back = lax.all_gather(w_out_b, "row", axis=0, tiled=True)
        d_hidden = lax.psum_scatter(contract_last(grad_b, w_out_back), "col", scatter_dimension=1, tiled=True)
        gelu_back = jax.vjp(gelu_tanh, pre_again)[1]
        d_pre = gelu_back(d_hidden)[0].astype(jnp.bfloat16)
        grad_x = lax.psum_scatter(contract_last(d_pre, w_in_cols), "col", scatter_dimension=1, tiled=True).astype(jnp.bfloat16)
        hidden_back = lax.all_gather(hidden_again, "col", axis=1, tiled=True)
        dw_out_layer = lax.psum_scatter(contract_first(hidden_back, grad_b), "row", scatter_dimension=0, tiled=True)
        dw_in_layer = lax.psum_scatter(contract_first(tok_full, d_pre), "row", scatter_dimension=0, tiled=True)
        grad_w_in = lax.psum(dw_in_layer, "depth")
        grad_w_out = lax.psum(dw_out_layer, "depth")
        return y_loc, grad_x, grad_w_in, grad_w_out

    return jax.shard_map(device_step, mesh=mesh, in_specs=(act_spec, weight_spec, weight_spec, act_spec), out_specs=(act_spec, act_spec, weight_spec, weight_spec), check_vma=False)
```

profile of v0, /device:TPU:0, one launch (start us, length us, event | category | flops | bytes accessed | tf_op | source)
XLA Modules:
  0.0 5490.0 jit_solution(6563729212545052207)
XLA Ops:
  7.2 0.7 all-gather.9.cloned.1.call-update
  7.9 0.7 all-gather.11.cloned.1.call-update
  8.7 0.7 all-gather.15.cloned.1.call-update
  9.4 105.2 %all-gather.9.cloned.1.call-done = bf16[2048,2048]{1,0:T(8,128)(2,1)} async-done(((bf16[2048,1024]{1,0:T(8,128)(2,1)}), bf16[2048,2048]{1,0:T(8,128)(2,1)}) %all-gather.9.cloned.1.call-update) | async-done | bytes 8388624 | tf_op jit(solution)/shard_map/all_gather | solution.py:20
  114.6 49.7 all-gather.11.cloned.1.call-done
  164.3 91.8 %fusion.14 = bf16[2048,8192]{1,0:T(8,128)(2,1)} fusion(bf16[2048,2048]{1,0:T(8,128)(2,1)} %all-gather.9.cloned.1.call-done, bf16[2048,8192]{1,0:T(8,128)(2,1)} %all-gather.11.cloned.1.call-done), kind=kOutput, calls=%fused_computation.17 | convolution fusion | flops 68870471680 | bytes 75497472 | tf_op jit(solution)/shard_map/dot_general | solution.py:22
  256.1 0.3 all-gather.17.cloned.1.call-start
  256.4 764.2 %all-gather.13.cloned.1.call-done = bf16[2048,16384]{1,0:T(8,128)(2,1)} async-done(((bf16[2048,8192]{1,0:T(8,128)(2,1)}), bf16[2048,16384]{1,0:T(8,128)(2,1)}) %all-gather.13.cloned.1.call-update) | async-done | bytes 67108880 | tf_op jit(solution)/shard_map/all_gather | solution.py:33
  1020.6 78.5 %convolution_convert_fusion = bf16[2048,1024]{1,0:T(8,128)(2,1)} fusion(bf16[2048,16384]{1,0:T(8,128)(2,1)} %all-gather.13.cloned.1.call-done, bf16[16384,1024]{1,0:T(8,128)(2,1)} %all-gather.15.cloned.1.call-done), kind=kOutput, calls=%fused_computation.19 | convolution fusion | flops 68721573888 | bytes 104857600 | tf_op jit(solution)/shard_map/dot_general | solution.py:35
  1099.1 0.5 all-gather.19.cloned.1.call-update
  1099.7 0.7 all-gather.21.cloned.1.call-update
  1100.5 46.9 all-gather.17.cloned.1.call-done
  1147.3 80.8 %fusion.15 = f32[2048,16384]{1,0:T(8,128)} fusion(bf16[2048,1024]{1,0:T(8,128)(2,1)} %param.7, bf16[16384,1024]{1,0:T(8,128)(2,1)} %all-gather.17.cloned.1.call-done), kind=kOutput, calls=%fused_computation.20 | convolution fusion | flops 68719476736 | bytes 171966464 | tf_op jit(solution)/shard_map/dot_general | solution.py:12
  1228.2 0.4 all-gather.23.cloned.1.call-start
  1228.7 23.5 all-gather.19.cloned.1.call-done
  1252.2 49.6 all-gather.21.cloned.1.call-done
  1301.8 1448.2 %reduce-scatter.5.cloned.1.call-done = f32[2048,8192]{1,0:T(8,128)} async-done(((f32[2048,16384]{1,0:T(8,128)}), f32[2048,8192]{1,0:T(8,128)}) %reduce-scatter.5.cloned.1.call-update) | async-done | bytes 67108880 | tf_op jit(solution)/shard_map/reduce_scatter | solution.py:40
  2750.0 126.2 %multiply_convert_fusion = (bf16[2048,8192]{1,0:T(8,128)(2,1)}, bf16[2048,8192]{1,0:T(8,128)(2,1)}) fusion(f32[2048,8192]{1,0:T(8,128)} %reduce-scatter.5.cloned.1.call-done, bf16[2048,2048]{1,0:T(8,128)(2,1)} %all-gather.19.cloned.1.call-done, bf16[2048,8192]{1,0:T(8,128)(2,1)} %all-gather.21.cloned.1.call-done), kind=kOutput, calls=%fused_computation.18 | convolution fusion | flops 69088575488 | bytes 176160768 | tf_op jit(solution)/shard_map/dot_general | solution.py:22
  2876.2 0.2 reduce-scatter.9.cloned.1.call-start
  2876.5 79.7 %fusion.17 = f32[2048,8192]{1,0:T(8,128)} fusion(bf16[2048,2048]{1,0:T(8,128)(2,1)} %all-gather.19.cloned.1.call-done, bf16[2048,8192]{1,0:T(8,128)(2,1)} %get-tuple-element.17), kind=kOutput, calls=%fused_computation.22 | convolution fusion | flops 68719476736 | bytes 109051904 | tf_op jit(solution)/shard_map/dot_general | solution.py:16
  2956.2 0.3 reduce-scatter.11.cloned.1.call-start
  2956.5 683.1 %all-gather.23.cloned.1.call-done = bf16[2048,16384]{1,0:T(8,128)(2,1)} async-done(((bf16[2048,8192]{1,0:T(8,128)(2,1)}), bf16[2048,16384]{1,0:T(8,128)(2,1)}) %all-gather.23.cloned.1.call-update) | async-done | bytes 67108880 | tf_op jit(solution)/shard_map/all_gather | solution.py:44
  3639.6 79.6 %fusion.18 = f32[16384,1024]{1,0:T(8,128)} fusion(bf16[2048,16384]{1,0:T(8,128)(2,1)} %all-gather.23.cloned.1.call-done, bf16[2048,1024]{1,0:T(8,128)(2,1)} %param.7), kind=kOutput, calls=%fused_computation.23 | convolution fusion | flops 68719476736 | bytes 138412032 | tf_op jit(solution)/shard_map/dot_general | solution.py:16
  3719.1 0.3 reduce-scatter.7.cloned.1.call-start
  3719.4 79.5 %fusion.16 = f32[2048,2048]{1,0:T(8,128)} fusion(bf16[2048,8192]{1,0:T(8,128)(2,1)} %get-tuple-element.17, bf16[2048,8192]{1,0:T(8,128)(2,1)} %all-gather.21.cloned.1.call-done), kind=kOutput, calls=%fused_computation.21 | convolution fusion | flops 68719476736 | bytes 83886080 | tf_op jit(solution)/shard_map/dot_general | solution.py:12
  3799.1 0.6 all-reduce.3.cloned.1.call-update
  3799.8 185.8 %reduce-scatter.7.cloned.1.call-done = f32[2048,1024]{1,0:T(8,128)} async-done(((f32[2048,2048]{1,0:T(8,128)}), f32[2048,1024]{1,0:T(8,128)}) %reduce-scatter.7.cloned.1.call-update) | async-done | bytes 8388624 | tf_op jit(solution)/shard_map/reduce_scatter | solution.py:43
  3985.6 6.1 convert_element_type.18
  3991.6 1447.9 %all-reduce.3.cloned.1.call-done = (f32[1024,8192]{1,0:T(8,128)}, f32[8192,1024]{1,0:T(8,128)}) async-done(((f32[1024,8192]{1,0:T(8,128)}, f32[8192,1024]{1,0:T(8,128)}), (f32[1024,8192]{1,0:T(8,128)}, f32[8192,1024]{1,0:T(8,128)})) %all-reduce.3.cloned.1.call-update) | async-done | bytes 67108880 | tf_op jit(solution)/shard_map/psum | solution.py:47
  5439.5 24.1 copy.10
  5463.6 7.7 copy-done
  5471.3 11.7 copy.11
  (19 shorter events, 0.5 us)
Async XLA Ops:
  7.2 107.5 %all-gather.9.cloned.1.call-start = ((), (), s32[]{:S(2)}) async-start(), calls=%async_computation.4 | async-start | bytes 12582912 | tf_op jit(solution)/shard_map/all_gather | solution.py:20
  7.9 156.4 %all-gather.11.cloned.1.call-start = ((), (), s32[]{:S(2)}) async-start(), calls=%async_computation.5 | async-start | bytes 50331648 | tf_op jit(solution)/shard_map/all_gather | solution.py:21
  8.6 247.8 %all-gather.15.cloned.1.call-start = ((), (), s32[]{:S(2)}) async-start(), calls=%async_computation.7 | async-start | bytes 50331648 | tf_op jit(solution)/shard_map/all_gather | solution.py:34
  9.4 1011.2 %all-gather.13.cloned.1.call-start = ((), (), s32[]{:S(2)}) async-start(), calls=%async_computation.6 | async-start | bytes 100663296 | tf_op jit(solution)/shard_map/all_gather | solution.py:33
  256.1 891.2 %all-gather.17.cloned.1.call-start = ((), (), s32[]{:S(2)}) async-start(), calls=%async_computation.8 | async-start | bytes 50331648 | tf_op jit(solution)/shard_map/all_gather | solution.py:39
  1099.1 153.1 %all-gather.19.cloned.1.call-start = ((), (), s32[]{:S(2)}) async-start(), calls=%async_computation.10 | async-start | bytes 12582912 | tf_op jit(solution)/shard_map/all_gather | solution.py:20
  1099.7 202.2 %all-gather.21.cloned.1.call-start = ((), (), s32[]{:S(2)}) async-start(), calls=%async_computation.11 | async-start | bytes 50331648 | tf_op jit(solution)/shard_map/all_gather | solution.py:21
  1100.4 1649.6 %reduce-scatter.5.cloned.1.call-start = ((), (), s32[]{:S(2)}) async-start(), calls=%async_computation.9 | async-start | bytes 201326592 | tf_op jit(solution)/shard_map/reduce_scatter | solution.py:40
  1228.2 2411.3 %all-gather.23.cloned.1.call-start = ((), (), s32[]{:S(2)}) async-start(), calls=%async_computation.14 | async-start | bytes 100663296 | tf_op jit(solution)/shard_map/all_gather | solution.py:44
  2876.2 922.8 %reduce-scatter.9.cloned.1.call-start = ((), (), s32[]{:S(2)}) async-start(), calls=%async_computation.13 | async-start | bytes 100663296 | tf_op jit(solution)/shard_map/reduce_scatter | solution.py:46
  2956.2 842.9 %reduce-scatter.11.cloned.1.call-start = ((), (), s32[]{:S(2)}) async-start(), calls=%async_computation.15 | async-start | bytes 100663296 | tf_op jit(solution)/shard_map/reduce_scatter | solution.py:45
  3719.1 266.4 %reduce-scatter.7.cloned.1.call-start = ((), (), s32[]{:S(2)}) async-start(), calls=%async_computation.12 | async-start | bytes 25165824 | tf_op jit(solution)/shard_map/reduce_scatter | solution.py:43
  3799.0 1640.5 %all-reduce.3.cloned.1.call-start = ((), (), s32[]{:S(2)}) async-start(), calls=%async_computation.16 | async-start | bytes 134217728 | tf_op jit(solution)/shard_map/psum | solution.py:47
  5439.5 31.8 copy-start
Sparse Core Ops, SparseCore 0:
  9.5 105.0 all-gather.8
  116.1 48.0 all-gather.10
  165.8 49.2 all-gather.14
  256.2 764.3 all-gather.12
  1099.2 48.0 all-gather.16
  1148.7 103.4 all-gather.18
  1253.7 48.0 all-gather.20
  1304.1 1445.8 reduce-scatter.4
  2876.4 763.1 all-gather.22
  3641.7 73.9 reduce-scatter.8
  3719.3 74.0 reduce-scatter.10
  3799.1 186.3 reduce-scatter.6
  3988.1 1451.4 all-reduce.2
where the time goes:
time: 5500 us; the launch traced here: 5490 us
  waiting for transfers between devices  4810 us (87%)
  matrix products  616 us (11%)
    reduce_scatter x1, waiting for transfers between devices, device_step(): lax.psum_scatter(contract_last(grad_b, w_out_back), 'col', scatter_dimens...  1450 us
    psum x1, waiting for transfers between devices, device_step(): grad_w_in = lax.psum(dw_in_layer, 'depth')  1450 us
    all_gather x1, waiting for transfers between devices, device_step(): hidden_full = lax.all_gather(hidden, 'col', axis=1, tiled=True)  764 us
    all_gather x1, waiting for transfers between devices, device_step(): hidden_back = lax.all_gather(hidden_again, 'col', axis=1, tiled=True)  683 us
    dot_general x2, matrix products, gather_pre(): pre_act = jnp.dot(tok_full, w_in_cols, preferred_element_type=jnp.float32)  218 us
    reduce_scatter x1, waiting for transfers between devices, device_step(): lax.psum_scatter(contract_last(d_pre, w_in_cols), 'col', scatter_dimensio...  186 us
    dot_general x2, matrix products, contract_last(): lax.dot_general(lhs, rhs, (((1,), (1,)), ((), ())), preferred_element_typ...  160 us
    dot_general x2, matrix products, contract_first(): lax.dot_general(lhs, rhs, (((0,), (0,)), ((), ())), preferred_element_typ...  159 us
  transfers between devices with their start and end apart: 13, of which 10 were waited for; matrix products, arithmetic and copies ran while one was open for 8% of the time, Pallas kernels for 0%

commit v1 on v0

v1 whole, which is shorter than its diff:
```python
import jax
import jax.numpy as jnp
from jax import lax
from jax.experimental import pallas as pl
from jax.experimental.pallas import tpu as pltpu
from jax.sharding import PartitionSpec as P


SWAP = [(0, 1), (1, 0)]


def gelu_tanh(pre_act):
    return jax.nn.gelu(pre_act, approximate=True)


def dot(lhs, rhs, lc, rc):
    return lax.dot_general(lhs, rhs, (((lc,), (rc,)), ((), ())), preferred_element_type=jnp.float32)


def part(arr, idx, size, axis):
    return lax.dynamic_slice_in_dim(arr, idx * size, size, axis)


def after(val, *deps):
    return lax.optimization_barrier((val,) + deps)[0]


def join_cols(mine, other, idx):
    rows, cols = mine.shape
    step = 256

    def body(idx_ref, mine_ref, other_ref, out_ref):
        @pl.when(idx_ref[0] == 0)
        def _():
            out_ref[:, :cols] = mine_ref[...]
            out_ref[:, cols:] = other_ref[...]

        @pl.when(idx_ref[0] != 0)
        def _():
            out_ref[:, :cols] = other_ref[...]
            out_ref[:, cols:] = mine_ref[...]

    return pl.pallas_call(
        body,
        out_shape=jax.ShapeDtypeStruct((rows, 2 * cols), mine.dtype),
        grid_spec=pltpu.PrefetchScalarGridSpec(
            num_scalar_prefetch=1,
            grid=(rows // step,),
            in_specs=[pl.BlockSpec((step, cols), lambda i, s: (i, 0))] * 2,
            out_specs=pl.BlockSpec((step, 2 * cols), lambda i, s: (i, 0)),
        ),
        cost_estimate=pl.CostEstimate(flops=rows * cols * 400, bytes_accessed=4 * rows * cols * mine.dtype.itemsize, transcendentals=0),
    )(idx[None], mine, other)


def lay_rows(pieces, places, n_rows, step):
    cols, dtype = pieces[0].shape[1], pieces[0].dtype
    sizes = [p.shape[0] // step for p in pieces]

    def body(place_ref, *refs):
        out_ref = refs[-1]
        at = pl.program_id(0)
        for k, size in enumerate(sizes):
            @pl.when((place_ref[k] >= 0) & (at >= place_ref[k]) & (at < place_ref[k] + size))
            def _(k=k):
                out_ref[...] = refs[k][...]

    def in_map(k, size):
        def index(at, place_ref):
            return (jnp.where(place_ref[k] < 0, 0, jnp.clip(at - place_ref[k], 0, size - 1)), 0)

        return index

    return pl.pallas_call(
        body,
        out_shape=jax.ShapeDtypeStruct((n_rows, cols), dtype),
        grid_spec=pltpu.PrefetchScalarGridSpec(
            num_scalar_prefetch=1,
            grid=(n_rows // step,),
            in_specs=[pl.BlockSpec((step, cols), in_map(k, size)) for k, size in enumerate(sizes)],
            out_specs=pl.BlockSpec((step, cols), lambda at, place_ref: (at, 0)),
        ),
        cost_estimate=pl.CostEstimate(flops=n_rows * cols * 400, bytes_accessed=2 * n_rows * cols * dtype.itemsize, transcendentals=0),
    )(places.astype(jnp.int32), *pieces)


def lay_dw2(own, own_core, oth, oth_core, stay, r, inner):
    step = 256
    whole = own.shape[0] // step
    piece = oth[0].shape[0] // step
    own_places = jnp.stack((whole * r, whole * (1 - r)))
    oth_places = jnp.concatenate((whole * r + piece * inner, whole * (1 - r) + piece * inner))
    places = jnp.concatenate((jnp.where(stay, own_places, -1), jnp.where(stay, -1, oth_places)))
    return lay_rows([own, own_core, *oth, *oth_core], places, 2 * own.shape[0], step)


def solution(mesh):
    act_spec = P(("depth", "row"), "col")
    weight_spec = P("row", "col")

    def step_body(tok, w_in, w_out, grad):
        d, c, r = lax.axis_index("depth"), lax.axis_index("col"), lax.axis_index("row")
        hid = tok.shape[1]
        ffn = w_in.shape[1] // 2
        half = ffn // 2

        def swap(v, axis):
            return lax.ppermute(v, axis, SWAP)

        def cores(v):
            return lax.all_gather(v, "row", axis=0, tiled=True)

        tok_x = swap(tok, "col")
        tok_y = swap(tok, "depth")
        tok_own = cores(tok)
        w1_cols = cores(w_in)
        w2_rows = cores(w_out)
        grad_own = cores(grad)
        w2_own = part(w2_rows, 2 * c + r, ffn, 0)
        w2_fwd = part(w2_rows, 4 * (1 - c) + 2 * r + d, half, 0)
        w2_a = swap(w2_fwd, "col")
        w2_b = swap(w2_a, "depth")
        grad_x = swap(after(grad, w2_fwd), "col")
        grad_y = swap(after(grad, w2_a), "depth")
        tok_xy = swap(tok_x, "depth")
        grad_xy = swap(grad_x, "depth")

        def w1_part(idx):
            return lax.dynamic_slice(w1_cols, (idx * hid, r * ffn), (hid, ffn))

        pre_own = dot(tok_own, w1_part(c), 1, 0)
        x_near = cores(join_cols(after(tok, pre_own), tok_x, c))
        pre = pre_own + dot(part(x_near, 1 - c, hid, 1), w1_part(1 - c), 1, 0)
        a_near = gelu_tanh(pre).astype(jnp.bfloat16)
        da_own = dot(w2_own, after(grad_own, a_near), 1, 1)
        y_own = dot(after(a_near, da_own), w2_own, 1, 0)
        dw2_near = dot(after(a_near, y_own), grad_own, 0, 0)
        w2_oth = lay_rows((w2_a, after(w2_b, dw2_near)), jnp.stack((d, 1 - d)) * (half // 512), ffn, 512)
        y_oth = dot(a_near, w2_oth, 1, 0)

        def over_cores(v):
            return lax.psum_scatter(v, "row", scatter_dimension=0, tiled=True)

        y_got = swap(over_cores(y_oth), "col")
        y_mine = over_cores(after(y_own, y_oth))
        g_near = cores(join_cols(after(grad, y_oth), grad_x, c))
        d_hidden = da_own.T + dot(part(g_near, 1 - c, hid, 1), w2_oth, 1, 1)
        du_near = jax.vjp(gelu_tanh, pre)[1](d_hidden)[0].astype(jnp.bfloat16)
        dx_oth = dot(du_near, w1_part(1 - c), 1, 1)
        dx_got = swap(over_cores(dx_oth), "col")
        dx_own = dot(after(du_near, dx_oth), w1_part(c), 1, 1)
        dx_mine = over_cores(dx_own)

        x_far = cores(join_cols(after(tok_y, a_near), tok_xy, c))
        w1 = part(w1_cols, r, ffn, 1)
        w2 = join_cols(w2_own, after(w2_oth, y_oth), c)
        pre_far = dot(after(x_far, dx_own), w1, 1, 0)
        a_far = gelu_tanh(pre_far).astype(jnp.bfloat16)
        g_far = cores(join_cols(after(grad_y, a_far), grad_xy, c))

        def dw1_near(idx, dep):
            return dot(part(after(x_near, dep), idx, hid, 1), du_near, 0, 0)

        def dw1_far(idx, dep):
            return dot(part(after(x_far, dep), idx, hid, 1), du_far, 0, 0)

        dw1_send_near = dw1_near(1 - r, a_far)
        du_far = jax.vjp(gelu_tanh, pre_far)[1](dot(after(g_far, dw1_send_near), w2, 1, 1))[0].astype(jnp.bfloat16)
        y = (y_mine + after(y_got, du_far)).astype(jnp.bfloat16)

        quarter, eighth = half // 2, half // 4
        sent, dep = [], y
        for q in range(2):
            at = 2 * d + q
            near = dot(part(after(a_near, dep), at, quarter, 1), part(g_near, 1 - c, hid, 1), 0, 0)
            dep = near + dot(part(a_far, at, quarter, 1), part(g_far, 1 - c, hid, 1), 0, 0)
            sent += [swap(dep[k * eighth:(k + 1) * eighth], "col") for k in range(2)]
        dw2_own = dw2_near + dot(after(a_far, dep), part(g_far, c, hid, 1), 0, 0)
        own_core = swap(dw2_own, "row")
        dw1_send = dw1_send_near + dw1_far(1 - r, dw2_own)
        dw1_got = swap(dw1_send, "row")
        dx = (dx_mine + after(dx_got, dw1_send)).astype(jnp.bfloat16)
        dw1_keep_near = dw1_near(r, dx)
        dw1_keep = dw1_keep_near + dw1_far(r, dw1_keep_near)
        dw1 = join_cols(dw1_keep, dw1_got, r)

        sent2 = [swap(v, "depth") for v in sent]
        oth = sent + sent2
        oth_core = [swap(v, "row") for v in oth]
        inner = jnp.concatenate((4 * d + jnp.arange(4), 4 - 4 * d + jnp.arange(4)))
        dw2 = lay_dw2(dw2_own, own_core, oth, oth_core, c == r, r, inner)
        return y, dx, dw1, dw2

    return jax.shard_map(step_body, mesh=mesh, in_specs=(act_spec, weight_spec, weight_spec, act_spec), out_specs=(act_spec, act_spec, weight_spec, weight_spec), check_vma=False)
```

time: 5500 us -> 2000 us (0.36)
  waiting for transfers between devices: 4810 us -> 818 us
  matrix products: 616 us -> 963 us
  Pallas kernels: 0 us -> 126 us
    all_gather x8, waiting for transfers between devices: 1720 us -> 67.6 us  [cores(): return lax.all_gather(v, 'row', axis=0, tiled=True)]
    reduce_scatter x4, waiting for transfers between devices: 1630 us -> 0.01 us  [over_cores(): return lax.psum_scatter(v, 'row', scatter_dimension=0, tiled=True)]
    psum x1 -> x0, waiting for transfers between devices: 1450 us -> none  [device_step(): grad_w_in = lax.psum(dw_in_layer, 'depth')]
    ppermute x0 -> x28, waiting for transfers between devices: none -> 747 us  [swap(): return lax.ppermute(v, axis, SWAP)]
    dot_general x7 -> x20, matrix products: 616 us -> 963 us  [dot(): lax.dot_general(lhs, rhs, (((lc,), (rc,)), ((), ())), preferred_element_t...]
    pallas_call x0 -> x8, Pallas kernels: none -> 126 us  [the longest x6 77.5 us: join_cols(): pl.pallas_call(body, out_shape=jax.ShapeDtypeStruct((rows, 2 * cols), min...]
  transfers between devices with their start and end apart: 13 -> 40, of which waited for: 10 -> 15; matrix products, arithmetic and copies ran while one was open for 8% -> 50% of each run, Pallas kernels for 0% -> 4%
where the time goes in v1:
time: 2000 us; the launch traced here: 1990 us
  matrix products  963 us (48%)
  waiting for transfers between devices  818 us (41%)
  Pallas kernels  126 us (6%)
  starting transfers between devices  24.4 us (1%)
  local copies, waits for them, and re-layouts  22.9 us (1%)
  other arithmetic  20.3 us (1%)
    dot_general x20, matrix products, dot(): lax.dot_general(lhs, rhs, (((lc,), (rc,)), ((), ())), preferred_element_t...  963 us
    ppermute x28, waiting for transfers between devices, swap(): return lax.ppermute(v, axis, SWAP)  747 us
    pallas_call x6, Pallas kernels, join_cols(): pl.pallas_call(body, out_shape=jax.ShapeDtypeStruct((rows, 2 * cols), min...  77.5 us
    all_gather x8, waiting for transfers between devices, cores(): return lax.all_gather(v, 'row', axis=0, tiled=True)  67.6 us
    pallas_call x2, Pallas kernels, lay_rows(): pl.pallas_call(body, out_shape=jax.ShapeDtypeStruct((n_rows, cols), dtype...  48 us
  transfers between devices with their start and end apart: 40, of which 15 were waited for; matrix products, arithmetic and copies ran while one was open for 50% of the time, Pallas kernels for 4%

profile of v1, /device:TPU:0, one launch (start us, length us, event | category | flops | bytes accessed | tf_op | source)
XLA Modules:
  0.0 1989.2 jit_solution(10714347974126022012)
XLA Ops:
  12.8 16.6 all-gather.11.cloned.1.call-done
  29.4 51.0 %all-gather.9.cloned.1.call-done = bf16[2048,8192]{1,0:T(8,128)(2,1)} async-done(((bf16[1024,8192]{1,0:T(8,128)(2,1)}), bf16[2048,8192]{1,0:T(8,128)(2,1)}) %all-gather.9.cloned.1.call-update) | async-done | bytes 33554448 | tf_op jit(solution)/shard_map/all_gather | solution.py:111
  80.3 49.2 %convolution_bitcast_fusion = f32[4096,4096]{0,1:T(8,128)} fusion(bf16[4096,1024]{1,0:T(8,128)(2,1)} %all-gather.11.cloned.1.call-done, bf16[2048,8192]{1,0:T(8,128)(2,1)} %all-gather.9.cloned.1.call-done, s32[]{:T(128)S(6)} %select_n.60, s32[]{:T(128)S(6)} %select_n.61), kind=kOutput, calls=%fused_computation.22 | convolution fusion | flops 34359738368 | bytes 83886088 | tf_op jit(solution)/shard_map/dot_general | solution.py:17
  157.8 79.2 %collective-permute-done.1.refs_0_ = bf16[2048,1024]{1,0:T(8,128)(2,1)} collective-permute-done((bf16[2048,1024]{1,0:T(8,128)(2,1)}, bf16[2048,1024]{1,0:T(8,128)(2,1)}, u32[]{:S(2)}, u32[]{:S(2)}) %collective-permute-start.1) | collective-permute-done | bytes 4194336 | tf_op jit(solution)/shard_map/ppermute | solution.py:108
  238.9 71.2 %multiply_convert_fusion.1 = (bf16[4096,4096]{0,1:T(8,128)(2,1)}, f32[4096,4096]{0,1:T(8,128)}) fusion(f32[4096,4096]{0,1:T(8,128)} %convolution_bitcast_fusion, bf16[2048,8192]{1,0:T(8,128)(2,1)} %all-gather.9.cloned.1.call-done, s32[]{:T(128)S(6)} %select_n.62, s32[]{:T(128)S(6)} %select_n.61, bf16[4096,2048]{1,0:T(8,128)(2,1)} %all-gather.13.cloned.1.call-done), kind=kOutput, calls=%fused_computation.20 | convolution fusion | flops 34527510528 | bytes 184550912 | tf_op jit(solution)/shard_map/dot_general | solution.py:17
  310.1 44.0 %fusion.75 = f32[4096,4096]{1,0:T(8,128)} fusion(bf16[4096,1024]{1,0:T(8,128)(2,1)} %constant_dynamic-slice_fusion.1.mine_ref, bf16[4096,1024]{1,0:T(8,128)(2,1)} %all-gather.17.cloned.1.call-done), kind=kOutput, calls=%fused_computation.86 | convolution fusion | flops 34359738368 | bytes 83886080 | tf_op jit(solution)/shard_map/dot_general | solution.py:17
  354.1 43.7 %fusion.76 = f32[4096,1024]{1,0:T(8,128)} fusion(bf16[4096,4096]{0,1:T(8,128)(2,1)} %get-tuple-element.46, bf16[4096,1024]{1,0:T(8,128)(2,1)} %constant_dynamic-slice_fusion.1.mine_ref), kind=kOutput, calls=%fused_computation.87 | convolution fusion | flops 34359738368 | bytes 58720256 | tf_op jit(solution)/shard_map/dot_general | solution.py:17
  397.8 42.9 %fusion.77 = f32[4096,1024]{1,0:T(8,128)} fusion(bf16[4096,4096]{0,1:T(8,128)(2,1)} %get-tuple-element.46, bf16[4096,1024]{1,0:T(8,128)(2,1)} %all-gather.17.cloned.1.call-done), kind=kOutput, calls=%fused_computation.88 | convolution fusion | flops 34359738368 | bytes 58720256 | tf_op jit(solution)/shard_map/dot_general | solution.py:17
  450.9 43.7 %fusion.78 = f32[4096,1024]{1,0:T(8,128)} fusion(bf16[4096,4096]{0,1:T(8,128)(2,1)} %get-tuple-element.46, bf16[4096,1024]{1,0:T(8,128)(2,1)} %shard_map.76.other_ref), kind=kOutput, calls=%fused_computation.89 | convolution fusion | flops 34359738368 | bytes 58720256 | tf_op jit(solution)/shard_map/dot_general | solution.py:17
  507.6 89.7 %collective-permute-done.5.mine_ref = bf16[2048,1024]{1,0:T(8,128)(2,1)} collective-permute-done((bf16[2048,1024]{1,0:T(8,128)(2,1)}, bf16[2048,1024]{1,0:T(8,128)(2,1)}, u32[]{:S(2)}, u32[]{:S(2)}) %collective-permute-start.5) | collective-permute-done | bytes 4194336 | tf_op jit(solution)/shard_map/ppermute | solution.py:108
  597.4 89.9 %collective-permute-done.6.other_ref = bf16[2048,1024]{1,0:T(8,128)(2,1)} collective-permute-done((bf16[2048,1024]{1,0:T(8,128)(2,1)}, bf16[2048,1024]{1,0:T(8,128)(2,1)}, u32[]{:S(2)}, u32[]{:S(2)}) %collective-permute-start.6) | collective-permute-done | bytes 4194336 | tf_op jit(solution)/shard_map/ppermute | solution.py:108
  696.3 86.4 %fusion.6 = bf16[4096,4096]{0,1:T(8,128)(2,1)} fusion(f32[4096,4096]{0,1:T(8,128)} %get-tuple-element.59, f32[4096,4096]{1,0:T(8,128)} %fusion.75, bf16[4096,1024]{1,0:T(8,128)(2,1)} %shard_map.76.other_ref, bf16[4096,2048]{1,0:T(8,128)(2,1)} %all-gather.21.cloned.1.call-done, s32[]{:T(128)S(6)} %select_n.62), kind=kOutput, calls=%fused_computation.10 | convolution fusion | flops 34712059904 | bytes 184549376 | tf_op jit(solution)/shard_map/dot_general | solution.py:17
  782.7 43.3 %fusion.42 = f32[4096,1024]{1,0:T(8,128)} fusion(bf16[4096,4096]{0,1:T(8,128)(2,1)} %fusion.6, bf16[2048,8192]{1,0:T(8,128)(2,1)} %all-gather.9.cloned.1.call-done, s32[]{:T(128)S(6)} %select_n.62, s32[]{:T(128)S(6)} %select_n.61), kind=kOutput, calls=%fused_computation.50 | convolution fusion | flops 34359738368 | bytes 58720264 | tf_op jit(solution)/shard_map/dot_general | solution.py:17
  826.0 43.4 %fusion.45 = f32[4096,1024]{1,0:T(8,128)} fusion(bf16[4096,4096]{0,1:T(8,128)(2,1)} %fusion.6, bf16[2048,8192]{1,0:T(8,128)(2,1)} %all-gather.9.cloned.1.call-done, s32[]{:T(128)S(6)} %select_n.60, s32[]{:T(128)S(6)} %select_n.61), kind=kOutput, calls=%fused_computation.53 | convolution fusion | flops 34359738368 | bytes 58720264 | tf_op jit(solution)/shard_map/dot_general | solution.py:17
  869.5 97.2 %multiply_convert_fusion = (bf16[4096,4096]{0,1:T(8,128)(2,1)}, f32[4096,4096]{0,1:T(8,128)}) fusion(bf16[4096,2048]{1,0:T(8,128)(2,1)} %all-gather.19.cloned.1.call-done, bf16[2048,8192]{1,0:T(8,128)(2,1)} %all-gather.9.cloned.1.call-done, s32[]{:T(128)S(6)} %select_n.61), kind=kOutput, calls=%fused_computation.19 | convolution fusion | flops 68870471680 | bytes 134217728 | tf_op jit(solution)/shard_map/dot_general | solution.py:17
  977.8 19.5 shard_map.80
  997.3 43.9 %fusion.31 = f32[1024,4096]{1,0:T(8,128)} fusion(bf16[4096,4096]{0,1:T(8,128)(2,1)} %fusion.6, bf16[4096,2048]{1,0:T(8,128)(2,1)} %all-gather.13.cloned.1.call-done, s32[]{:T(128)S(6)} %select_n.65), kind=kOutput, calls=%fused_computation.43 | convolution fusion | flops 34359738368 | bytes 58720260 | tf_op jit(solution)/shard_map/dot_general | solution.py:17
  1042.3 120.5 %fusion.13 = bf16[4096,4096]{0,1:T(8,128)(2,1)} fusion(f32[4096,4096]{0,1:T(8,128)} %get-tuple-element.61, bf16[4096,2048]{1,0:T(8,128)(2,1)} %all-gather.23.cloned.1.call-done, bf16[4096,2048]{1,0:T(8,128)(2,1)} %shard_map.80), kind=kOutput, calls=%fused_computation.17 | convolution fusion | flops 69055021056 | bytes 134217728 | tf_op jit(solution)/shard_map/dot_general | solution.py:17
  1162.8 55.6 %collective-permute-done.3 = f32[2048,1024]{1,0:T(8,128)} collective-permute-done((f32[2048,1024]{1,0:T(8,128)}, f32[2048,1024]{1,0:T(8,128)}, u32[]{:S(2)}, u32[]{:S(2)}) %collective-permute-start.3) | collective-permute-done | bytes 8388640 | tf_op jit(solution)/shard_map/ppermute | solution.py:108
  1271.6 16.0 fusion.56
  1287.6 43.7 %convolution_add_fusion.1.refs_0_ = f32[4096,1024]{1,0:T(8,128)} fusion(f32[4096,1024]{1,0:T(8,128)} %fusion.77, bf16[4096,4096]{0,1:T(8,128)(2,1)} %get-tuple-element.47, bf16[4096,2048]{1,0:T(8,128)(2,1)} %all-gather.23.cloned.1.call-done, s32[]{:T(128)S(6)} %select_n.60), kind=kOutput, calls=%fused_computation.25 | convolution fusion | flops 34363932672 | bytes 75497472 | tf_op jit(solution)/shard_map/dot_general | solution.py:17
  1331.2 43.3 %fusion.34 = f32[1024,4096]{1,0:T(8,128)} fusion(f32[1024,4096]{1,0:T(8,128)} %fusion.31, bf16[4096,4096]{0,1:T(8,128)(2,1)} %fusion.13, bf16[4096,2048]{1,0:T(8,128)(2,1)} %all-gather.19.cloned.1.call-done, s32[]{:T(128)S(6)} %select_n.65), kind=kOutput, calls=%fused_computation.46 | convolution fusion | flops 34363932672 | bytes 75497472 | tf_op jit(solution)/shard_map/dot_general | solution.py:17
  1383.7 219.3 %collective-permute-done.15.refs_5_ = f32[512,1024]{1,0:T(8,128)S(1)} collective-permute-done((f32[512,1024]{1,0:T(8,128)S(1)}, f32[512,1024]{1,0:T(8,128)S(1)}, u32[]{:S(2)}, u32[]{:S(2)}) %collective-permute-start.15) | collective-permute-done | bytes 2097184 | tf_op jit(solution)/shard_map/ppermute | solution.py:108
  1604.6 43.3 %collective-permute-done.14.refs_4_ = f32[512,1024]{1,0:T(8,128)S(1)} collective-permute-done((f32[512,1024]{1,0:T(8,128)S(1)}, f32[512,1024]{1,0:T(8,128)S(1)}, u32[]{:S(2)}, u32[]{:S(2)}) %collective-permute-start.14) | collective-permute-done | bytes 2097184 | tf_op jit(solution)/shard_map/ppermute | solution.py:108
  1647.9 45.0 %collective-permute-done.13.refs_3_ = f32[512,1024]{1,0:T(8,128)} collective-permute-done((f32[512,1024]{1,0:T(8,128)S(1)}, f32[512,1024]{1,0:T(8,128)}, u32[]{:S(2)}, u32[]{:S(2)}) %collective-permute-start.13) | collective-permute-done | bytes 2097184 | tf_op jit(solution)/shard_map/ppermute | solution.py:108
  1694.0 43.5 %collective-permute-done.12.refs_2_ = f32[512,1024]{1,0:T(8,128)} collective-permute-done((f32[512,1024]{1,0:T(8,128)S(1)}, f32[512,1024]{1,0:T(8,128)}, u32[]{:S(2)}, u32[]{:S(2)}) %collective-permute-start.12) | collective-permute-done | bytes 2097184 | tf_op jit(solution)/shard_map/ppermute | solution.py:108
  1766.9 21.4 %collective-permute-done.18.refs_8_ = f32[512,1024]{1,0:T(8,128)} collective-permute-done((f32[512,1024]{1,0:T(8,128)S(1)}, f32[512,1024]{1,0:T(8,128)}, u32[]{:S(2)}, u32[]{:S(2)}) %collective-permute-start.18) | collective-permute-done | bytes 2097184 | tf_op jit(solution)/shard_map/ppermute | solution.py:108
  1789.3 43.5 %fusion.18 = f32[1024,4096]{1,0:T(8,128)} fusion(bf16[4096,4096]{0,1:T(8,128)(2,1)} %fusion.6, bf16[4096,2048]{1,0:T(8,128)(2,1)} %all-gather.13.cloned.1.call-done, s32[]{:T(128)S(6)} %select_n.68), kind=kOutput, calls=%fused_computation.28 | convolution fusion | flops 34359738368 | bytes 58720260 | tf_op jit(solution)/shard_map/dot_general | solution.py:17
  1833.7 43.1 %collective-permute-done.16.refs_6_ = f32[512,1024]{1,0:T(8,128)} collective-permute-done((f32[512,1024]{1,0:T(8,128)}, f32[512,1024]{1,0:T(8,128)}, u32[]{:S(2)}, u32[]{:S(2)}) %collective-permute-start.16) | collective-permute-done | bytes 2097184 | tf_op jit(solution)/shard_map/ppermute | solution.py:108
  1877.3 43.3 %fusion.37.mine_ref = f32[1024,4096]{1,0:T(8,128)} fusion(f32[1024,4096]{1,0:T(8,128)} %fusion.18, bf16[4096,4096]{0,1:T(8,128)(2,1)} %fusion.13, bf16[4096,2048]{1,0:T(8,128)(2,1)} %all-gather.19.cloned.1.call-done, s32[]{:T(128)S(6)} %select_n.68), kind=kOutput, calls=%fused_computation.47 | convolution fusion | flops 34363932672 | bytes 75497472 | tf_op jit(solution)/shard_map/dot_general | solution.py:17
  1920.6 22.3 %shard_map.81 = f32[1024,8192]{1,0:T(8,128)} custom-call(s32[1]{0:T(128)} %bitcast.5.idx_ref, f32[1024,4096]{1,0:T(8,128)} %fusion.37.mine_ref, f32[1024,4096]{1,0:T(8,128)} %collective-permute-done.10.other_ref), custom_call_target="tpu_custom_call" | custom-call | flops 1677721600 | bytes 67108864 | tf_op jit(solution)/shard_map/pallas_call | solution.py:43
  1944.3 37.8 %shard_map.82 = f32[8192,1024]{1,0:T(8,128)} custom-call(s32[18]{0:T(128)} %pad_add_fusion.place_ref, f32[4096,1024]{1,0:T(8,128)} %convolution_add_fusion.1.refs_0_, f32[4096,1024]{1,0:T(8,128)} %collective-permute-done.11.refs_1_, f32[512,1024]{1,0:T(8,128)} %collective-permute-done.12.refs_2_, f32[512,1024]{1,0:T(8,128)} %collective-permute-done.13.refs_3_, ...), custom_call_target="tpu_custom_call" | custom-call | flops 3355443200 | bytes 67108864 | tf_op jit(solution)/shard_map/pallas_call | solution.py:74
  (119 shorter events, 178.1 us)
Async XLA Ops:
  7.9 72.5 %all-gather.9.cloned.1.call-start = ((), (), s32[]{:S(2)}) async-start(), calls=%async_computation.4 | async-start | bytes 50331648 | tf_op jit(solution)/shard_map/all_gather | solution.py:111
  8.6 129.9 %all-gather.15.cloned.1.call-start = ((), (), s32[]{:S(2)}) async-start(), calls=%async_computation.7 | async-start | bytes 50331648 | tf_op jit(solution)/shard_map/all_gather | solution.py:111
  9.4 229.5 %all-gather.13.cloned.1.call-start = ((), (), s32[]{:S(2)}) async-start(), calls=%async_computation.6 | async-start | bytes 25165824 | tf_op jit(solution)/shard_map/all_gather | solution.py:111
  9.4 120.2 %collective-permute-start = (bf16[2048,1024]{1,0:T(8,128)(2,1)}, bf16[2048,1024]{1,0:T(8,128)(2,1)}, u32[]{:S(2)}, u32[]{:S(2)}) collective-permute-start(bf16[2048,1024]{1,0:T(8,128)(2,1)} %mine_ref), channel_id=1, source_target_pairs={{0,2},{2,0},{1,3},{3,1},{4,6},{6,4},{5,7},{7,5}} | collective-permute-start | bytes 12582920 | tf_op jit(solution)/shard_map/ppermute | solution.py:108
  138.5 171.6 %all-gather.17.cloned.1.call-start = ((), (), s32[]{:S(2)}) async-start(), calls=%async_computation.8 | async-start | bytes 12582912 | tf_op jit(solution)/shard_map/all_gather | solution.py:111
  143.2 93.8 %collective-permute-start.1 = (bf16[2048,1024]{1,0:T(8,128)(2,1)}, bf16[2048,1024]{1,0:T(8,128)(2,1)}, u32[]{:S(2)}, u32[]{:S(2)}) collective-permute-start(bf16[2048,1024]{1,0:T(8,128)(2,1)} %constant_dynamic-slice_fusion), channel_id=1, source_target_pairs={{0,2},{2,0},{1,3},{3,1},{4,6},{6,4},{5,7},{7,5}} | collective-permute-start | bytes 12582920 | tf_op jit(solution)/shard_map/ppermute | solution.py:108
  145.0 551.3 %all-gather.21.cloned.1.call-start = ((), (), s32[]{:S(2)}) async-start(), calls=%async_computation.12 | async-start | bytes 25165824 | tf_op jit(solution)/shard_map/all_gather | solution.py:111
  146.1 348.5 %collective-permute-start.7 = (bf16[2048,1024]{1,0:T(8,128)(2,1)}, bf16[2048,1024]{1,0:T(8,128)(2,1)}, u32[]{:S(2)}, u32[]{:S(2)}) collective-permute-start(bf16[2048,1024]{1,0:T(8,128)(2,1)} %mine_ref.1), channel_id=1, source_target_pairs={{0,2},{2,0},{1,3},{3,1},{4,6},{6,4},{5,7},{7,5}} | collective-permute-start | bytes 12582920 | tf_op jit(solution)/shard_map/ppermute | solution.py:108
  237.0 203.7 %collective-permute-start.2 = (bf16[2048,1024]{1,0:T(8,128)(2,1)}, bf16[2048,1024]{1,0:T(8,128)(2,1)}, u32[]{:S(2)}, u32[]{:S(2)}) collective-permute-start(bf16[2048,1024]{1,0:T(8,128)(2,1)} %collective-permute-done.1.refs_0_), channel_id=1, source_target_pairs={{0,4},{4,0},{1,5},{5,1},{2,6},{6,2},{3,7},{7,3}} | collective-permute-start | bytes 12582920 | tf_op jit(solution)/shard_map/ppermute | solution.py:108
  503.5 365.9 %all-gather.19.cloned.1.call-start = ((), (), s32[]{:S(2)}) async-start(), calls=%async_computation.11 | async-start | bytes 25165824 | tf_op jit(solution)/shard_map/all_gather | solution.py:111
  503.6 93.8 %collective-permute-start.5 = (bf16[2048,1024]{1,0:T(8,128)(2,1)}, bf16[2048,1024]{1,0:T(8,128)(2,1)}, u32[]{:S(2)}, u32[]{:S(2)}) collective-permute-start(bf16[2048,1024]{1,0:T(8,128)(2,1)} %mine_ref), channel_id=1, source_target_pairs={{0,4},{4,0},{1,5},{5,1},{2,6},{6,2},{3,7},{7,3}} | collective-permute-start | bytes 12582920 | tf_op jit(solution)/shard_map/ppermute | solution.py:108
  503.8 183.4 %collective-permute-start.6 = (bf16[2048,1024]{1,0:T(8,128)(2,1)}, bf16[2048,1024]{1,0:T(8,128)(2,1)}, u32[]{:S(2)}, u32[]{:S(2)}) collective-permute-start(bf16[2048,1024]{1,0:T(8,128)(2,1)} %collective-permute-done.other_ref), channel_id=1, source_target_pairs={{0,4},{4,0},{1,5},{5,1},{2,6},{6,2},{3,7},{7,3}} | collective-permute-start | bytes 12582920 | tf_op jit(solution)/shard_map/ppermute | solution.py:108
  505.6 461.1 %collective-permute-start.4 = (bf16[2048,1024]{1,0:T(8,128)(2,1)}, bf16[2048,1024]{1,0:T(8,128)(2,1)}, u32[]{:S(2)}, u32[]{:S(2)}) collective-permute-start(bf16[2048,1024]{1,0:T(8,128)(2,1)} %mine_ref.1), channel_id=1, source_target_pairs={{0,4},{4,0},{1,5},{5,1},{2,6},{6,2},{3,7},{7,3}} | collective-permute-start | bytes 12582920 | tf_op jit(solution)/shard_map/ppermute | solution.py:108
  505.8 460.9 %collective-permute-start.8 = (bf16[2048,1024]{1,0:T(8,128)(2,1)}, bf16[2048,1024]{1,0:T(8,128)(2,1)}, u32[]{:S(2)}, u32[]{:S(2)}) collective-permute-start(bf16[2048,1024]{1,0:T(8,128)(2,1)} %collective-permute-done.7.other_ref), channel_id=1, source_target_pairs={{0,4},{4,0},{1,5},{5,1},{2,6},{6,2},{3,7},{7,3}} | collective-permute-start | bytes 12582920 | tf_op jit(solution)/shard_map/ppermute | solution.py:108
  696.2 345.0 %all-gather.23.cloned.1.call-start = ((), (), s32[]{:S(2)}) async-start(), calls=%async_computation.13 | async-start | bytes 25165824 | tf_op jit(solution)/shard_map/all_gather | solution.py:111
  976.4 242.0 %reduce-scatter.5.cloned.1.call-start = ((), (), s32[]{:S(2)}) async-start(), calls=%async_computation.9 | async-start | bytes 25165824 | tf_op jit(solution)/shard_map/reduce_scatter | solution.py:142
  977.0 397.5 %reduce-scatter.11.cloned.1.call-start = ((), (), s32[]{:S(2)}) async-start(), calls=%async_computation.15 | async-start | bytes 25165824 | tf_op jit(solution)/shard_map/reduce_scatter | solution.py:142
  977.7 764.2 %reduce-scatter.9.cloned.1.call-start = ((), (), s32[]{:S(2)}) async-start(), calls=%async_computation.14 | async-start | bytes 25165824 | tf_op jit(solution)/shard_map/reduce_scatter | solution.py:142
  1041.2 177.2 %collective-permute-start.3 = (f32[2048,1024]{1,0:T(8,128)}, f32[2048,1024]{1,0:T(8,128)}, u32[]{:S(2)}, u32[]{:S(2)}) collective-permute-start(f32[2048,1024]{1,0:T(8,128)} %reduce-scatter.7.cloned.1.call-done), channel_id=1, source_target_pairs={{0,2},{2,0},{1,3},{3,1},{4,6},{6,4},{5,7},{7,5}} | collective-permute-start | bytes 25165832 | tf_op jit(solution)/shard_map/ppermute | solution.py:108
  1374.5 502.3 %collective-permute-start.10 = (f32[1024,4096]{1,0:T(8,128)}, f32[1024,4096]{1,0:T(8,128)}, u32[]{:S(2)}, u32[]{:S(2)}) collective-permute-start(f32[1024,4096]{1,0:T(8,128)} %fusion.34), channel_id=1, source_target_pairs={{0,1},{1,0},{2,3},{3,2},{4,5},{5,4},{6,7},{7,6}} | collective-permute-start | bytes 50331656 | tf_op jit(solution)/shard_map/ppermute | solution.py:108
  1374.5 366.6 %collective-permute-start.9 = (f32[2048,1024]{1,0:T(8,128)}, f32[2048,1024]{1,0:T(8,128)}, u32[]{:S(2)}, u32[]{:S(2)}) collective-permute-start(f32[2048,1024]{1,0:T(8,128)} %reduce-scatter.11.cloned.1.call-done), channel_id=1, source_target_pairs={{0,2},{2,0},{1,3},{3,1},{4,6},{6,4},{5,7},{7,5}} | collective-permute-start | bytes 25165832 | tf_op jit(solution)/shard_map/ppermute | solution.py:108
  1378.7 224.3 %collective-permute-start.15 = (f32[512,1024]{1,0:T(8,128)S(1)}, f32[512,1024]{1,0:T(8,128)S(1)}, u32[]{:S(2)}, u32[]{:S(2)}) collective-permute-start(f32[512,1024]{1,0:T(8,128)S(1)} %get-tuple-element.52), channel_id=1, source_target_pairs={{0,2},{2,0},{1,3},{3,1},{4,6},{6,4},{5,7},{7,5}} | collective-permute-start | bytes 6291464 | tf_op jit(solution)/shard_map/ppermute | solution.py:108
  1381.6 266.3 %collective-permute-start.14 = (f32[512,1024]{1,0:T(8,128)S(1)}, f32[512,1024]{1,0:T(8,128)S(1)}, u32[]{:S(2)}, u32[]{:S(2)}) collective-permute-start(f32[512,1024]{1,0:T(8,128)S(1)} %get-tuple-element.53), channel_id=1, source_target_pairs={{0,2},{2,0},{1,3},{3,1},{4,6},{6,4},{5,7},{7,5}} | collective-permute-start | bytes 6291464 | tf_op jit(solution)/shard_map/ppermute | solution.py:108
  1383.3 309.7 %collective-permute-start.13 = (f32[512,1024]{1,0:T(8,128)S(1)}, f32[512,1024]{1,0:T(8,128)}, u32[]{:S(2)}, u32[]{:S(2)}) collective-permute-start(f32[512,1024]{1,0:T(8,128)S(1)} %get-tuple-element.54), channel_id=1, source_target_pairs={{0,2},{2,0},{1,3},{3,1},{4,6},{6,4},{5,7},{7,5}} | collective-permute-start | bytes 6291464 | tf_op jit(solution)/shard_map/ppermute | solution.py:108
  1603.0 134.4 %collective-permute-start.12 = (f32[512,1024]{1,0:T(8,128)S(1)}, f32[512,1024]{1,0:T(8,128)}, u32[]{:S(2)}, u32[]{:S(2)}) collective-permute-start(f32[512,1024]{1,0:T(8,128)S(1)} %get-tuple-element.55), channel_id=1, source_target_pairs={{0,2},{2,0},{1,3},{3,1},{4,6},{6,4},{5,7},{7,5}} | collective-permute-start | bytes 6291464 | tf_op jit(solution)/shard_map/ppermute | solution.py:108
  1647.9 89.5 %collective-permute-start.23 = (f32[512,1024]{1,0:T(8,128)S(1)}, f32[512,1024]{1,0:T(8,128)S(1)}, u32[]{:S(2)}, u32[]{:S(2)}) collective-permute-start(f32[512,1024]{1,0:T(8,128)S(1)} %collective-permute-done.15.refs_5_), channel_id=1, source_target_pairs={{0,1},{1,0},{2,3},{3,2},{4,5},{5,4},{6,7},{7,6}} | collective-permute-start | bytes 6291464 | tf_op jit(solution)/shard_map/ppermute | solution.py:108
  1737.4 205.5 %collective-permute-start.11 = (f32[4096,1024]{1,0:T(8,128)}, f32[4096,1024]{1,0:T(8,128)}, u32[]{:S(2)}, u32[]{:S(2)}) collective-permute-start(f32[4096,1024]{1,0:T(8,128)} %convolution_add_fusion.1.refs_0_), channel_id=1, source_target_pairs={{0,1},{1,0},{2,3},{3,2},{4,5},{5,4},{6,7},{7,6}} | collective-permute-start | bytes 50331656 | tf_op jit(solution)/shard_map/ppermute | solution.py:108
  1765.9 67.3 %collective-permute-start.17 = (f32[512,1024]{1,0:T(8,128)}, f32[512,1024]{1,0:T(8,128)}, u32[]{:S(2)}, u32[]{:S(2)}) collective-permute-start(f32[512,1024]{1,0:T(8,128)} %collective-permute-done.13.refs_3_), channel_id=1, source_target_pairs={{0,4},{4,0},{1,5},{5,1},{2,6},{6,2},{3,7},{7,3}} | collective-permute-start | bytes 6291464 | tf_op jit(solution)/shard_map/ppermute | solution.py:108
  1788.3 88.5 %collective-permute-start.16 = (f32[512,1024]{1,0:T(8,128)}, f32[512,1024]{1,0:T(8,128)}, u32[]{:S(2)}, u32[]{:S(2)}) collective-permute-start(f32[512,1024]{1,0:T(8,128)} %collective-permute-done.12.refs_2_), channel_id=1, source_target_pairs={{0,4},{4,0},{1,5},{5,1},{2,6},{6,2},{3,7},{7,3}} | collective-permute-start | bytes 6291464 | tf_op jit(solution)/shard_map/ppermute | solution.py:108
  1833.2 109.7 %collective-permute-start.27 = (f32[512,1024]{1,0:T(8,128)}, f32[512,1024]{1,0:T(8,128)S(1)}, u32[]{:S(2)}, u32[]{:S(2)}) collective-permute-start(f32[512,1024]{1,0:T(8,128)} %copy-done.3), channel_id=1, source_target_pairs={{0,1},{1,0},{2,3},{3,2},{4,5},{5,4},{6,7},{7,6}} | collective-permute-start | bytes 6291464 | tf_op jit(solution)/shard_map/ppermute | solution.py:108
  1833.2 109.7 %collective-permute-start.26 = (f32[512,1024]{1,0:T(8,128)}, f32[512,1024]{1,0:T(8,128)}, u32[]{:S(2)}, u32[]{:S(2)}) collective-permute-start(f32[512,1024]{1,0:T(8,128)} %collective-permute-done.18.refs_8_), channel_id=1, source_target_pairs={{0,1},{1,0},{2,3},{3,2},{4,5},{5,4},{6,7},{7,6}} | collective-permute-start | bytes 6291464 | tf_op jit(solution)/shard_map/ppermute | solution.py:108
  1876.8 66.2 %collective-permute-start.24 = (f32[512,1024]{1,0:T(8,128)}, f32[512,1024]{1,0:T(8,128)}, u32[]{:S(2)}, u32[]{:S(2)}) collective-permute-start(f32[512,1024]{1,0:T(8,128)} %collective-permute-done.16.refs_6_), channel_id=1, source_target_pairs={{0,1},{1,0},{2,3},{3,2},{4,5},{5,4},{6,7},{7,6}} | collective-permute-start | bytes 6291464 | tf_op jit(solution)/shard_map/ppermute | solution.py:108
  (17 other events, 758.0 us)
Sparse Core Ops, SparseCore 0:
  9.5 19.8 all-gather.10
  30.9 49.4 all-gather.8
  81.9 49.4 all-gather.14
  138.6 28.5 all-gather.12
  168.6 18.2 all-gather.16
  503.6 27.2 all-gather.20
  696.3 27.2 all-gather.18
  975.8 27.0 all-gather.22
  1005.1 23.3 reduce-scatter.6
  1030.7 23.5 reduce-scatter.4
  1056.6 23.5 reduce-scatter.10
  1082.3 23.5 reduce-scatter.8

commit v2 on v0

v2 whole, which is shorter than its diff:
```python
import jax
import jax.numpy as jnp
from jax import lax
from jax.experimental import pallas as pl
from jax.experimental.pallas import tpu as pltpu
from jax.sharding import PartitionSpec as P


SWAP = [(0, 1), (1, 0)]


def gelu_tanh(pre_act):
    return jax.nn.gelu(pre_act, approximate=True)


def dot(lhs, rhs, lc, rc):
    return lax.dot_general(lhs, rhs, (((lc,), (rc,)), ((), ())), preferred_element_type=jnp.float32)


def part(arr, idx, size, axis):
    return lax.dynamic_slice_in_dim(arr, idx * size, size, axis)


def after(val, *deps):
    return lax.optimization_barrier((val,) + deps)[0]


def lay(pieces, out_rows, out_cols, step, first=None, blocks=None, onto=None):
    cols, dtype = out_cols, pieces[0][0].dtype
    width = next(iter({p[4][1] for p in pieces}))
    per_col = out_rows // step
    sizes = [p[2] // step for p in pieces]
    n = len(pieces)
    table = [p[1] for p in pieces] + [p[3] // step for p in pieces] + [p[4][0] for p in pieces]
    runs = 0
    if onto is not None:
        table += list(first)
        runs = blocks
        total = len(first) * blocks
    else:
        total = per_col * (cols // width)
    table = jnp.stack([jnp.asarray(v, jnp.int32) for v in table])

    def where_to(at, tab):
        if onto is None:
            return at
        pos = tab[3 * n] + at
        for k in range(1, len(first)):
            pos = jnp.where(at >= k * runs, tab[3 * n + k] + at - k * runs, pos)
        return pos

    def body(tab, *refs):
        out_ref = refs[-1]
        pos = where_to(pl.program_id(0), tab)
        for k, size in enumerate(sizes):
            @pl.when((tab[k] >= 0) & (pos >= tab[k]) & (pos < tab[k] + size))
            def _(k=k):
                out_ref[...] = refs[k][...]

    def in_map(k, size):
        def index(at, tab):
            here = jnp.where(tab[k] < 0, 0, jnp.clip(where_to(at, tab) - tab[k], 0, size - 1))
            return (tab[n + k] + here, tab[2 * n + k])

        return index

    def out_map(at, tab):
        pos = where_to(at, tab)
        return (lax.rem(pos, per_col), lax.div(pos, per_col))

    in_specs = [pl.BlockSpec((step, width), in_map(k, size)) for k, size in enumerate(sizes)]
    operands = [p[0] for p in pieces]
    aliases = {}
    if onto is not None:
        in_specs.append(pl.BlockSpec(memory_space=pl.ANY))
        operands.append(onto)
        aliases = {n + 1: 0}
    return pl.pallas_call(
        body,
        out_shape=jax.ShapeDtypeStruct((out_rows, out_cols), dtype),
        grid_spec=pltpu.PrefetchScalarGridSpec(
            num_scalar_prefetch=1,
            grid=(total,),
            in_specs=in_specs,
            out_specs=pl.BlockSpec((step, width), out_map),
        ),
        input_output_aliases=aliases,
        cost_estimate=pl.CostEstimate(flops=total * step * width * 400, bytes_accessed=2 * total * step * width * dtype.itemsize, transcendentals=0),
    )(table, *operands)


def whole(arr, place):
    return (arr, place, arr.shape[0], 0, (0, arr.shape[1]))


def join_cols(mine, other, idx, step):
    per = mine.shape[0] // step
    return lay([whole(mine, idx * per), whole(other, (1 - idx) * per)], mine.shape[0], 2 * mine.shape[1], step)


def solution(mesh):
    act_spec = P(("depth", "row"), "col")
    weight_spec = P("row", "col")

    def step_body(tok, w_in, w_out, grad):
        d, c, r = lax.axis_index("depth"), lax.axis_index("col"), lax.axis_index("row")
        hid = tok.shape[1]
        ffn = w_in.shape[1] // 2
        half, quarter, eighth = ffn // 2, ffn // 4, ffn // 8
        stay = c == r

        def swap(v, axis):
            return lax.ppermute(v, axis, SWAP)

        def cores(v):
            return lax.all_gather(v, "row", axis=0, tiled=True)

        def over_cores(v):
            return lax.psum_scatter(v, "row", scatter_dimension=0, tiled=True)

        tok_x = swap(tok, "col")
        tok_y = swap(tok, "depth")
        tok_own = cores(tok)
        grad_own = cores(grad)

        w2_cut = part(w_out, 1 - r, ffn, 0)
        w1_cut = part(w_in, 1 - r, ffn, 1)
        w2_core = swap(w2_cut, "row")
        w1_core = swap(w1_cut, "row")
        step = 512
        w2_fwd = lay([(w_out, jnp.where(stay, -1, 0), half, r * ffn + d * half, (0, hid)), (w2_core, jnp.where(stay, 0, -1), half, d * half, (0, hid))], half, hid, step)
        per1 = hid // 256
        w1 = lay([(w_in, r * per1, hid, 0, (r, ffn)), whole(w1_core, (1 - r) * per1)], 2 * hid, ffn, 256)
        w2_a = swap(w2_fwd, "col")
        grad_x = swap(after(grad, w2_fwd), "col")
        tok_xy = swap(tok_x, "depth")
        w2_b = swap(w2_a, "depth")
        grad_y = swap(after(grad, w2_a), "depth")
        grad_xy = swap(grad_x, "depth")

        def with_slope(pre):
            hidden, back = jax.vjp(gelu_tanh, pre)
            return hidden.astype(jnp.bfloat16), back(jnp.ones_like(pre))[0]

        pre_own = dot(tok_own, part(w1, c, hid, 0), 1, 0)
        tok_oth = cores(after(tok_x, pre_own))
        w2_own = lay([(w_out, jnp.where(stay, 0, -1), ffn, r * ffn, (0, hid)), (after(w2_core, pre_own), jnp.where(stay, -1, 0), ffn, 0, (0, hid))], ffn, hid, step)
        pre = pre_own + dot(after(tok_oth, w2_own), part(w1, 1 - c, hid, 0), 1, 0)
        a_near, slope_near = lax.optimization_barrier(with_slope(pre))
        x_far = cores(join_cols(after(tok_y, a_near), tok_xy, c, step))
        da_own = dot(w2_own, after(grad_own, a_near), 1, 1)
        x_near = cores(join_cols(after(tok, da_own), tok_x, c, step))
        a_far, slope_far = lax.optimization_barrier(with_slope(dot(after(x_far, da_own), w1, 1, 0)))
        per2 = ffn // step
        w2 = lay([whole(w2_own, c * per2), whole(w2_a, (1 - c) * per2 + d * (per2 // 2)), whole(after(w2_b, a_far), (1 - c) * per2 + (1 - d) * (per2 // 2))], ffn, 2 * hid, step)
        y_oth = dot(a_near, part(w2, 1 - c, hid, 1), 1, 0)
        y_got = swap(over_cores(y_oth), "col")
        grad_oth = cores(after(grad_x, y_oth))
        d_hidden = da_own.T + dot(grad_oth, part(w2, 1 - c, hid, 1), 1, 1)
        du_near = (slope_near * d_hidden).astype(jnp.bfloat16)
        dx_oth = dot(du_near, part(w1, 1 - c, hid, 0), 1, 1)
        dx_got = swap(over_cores(dx_oth), "col")
        g_far = cores(join_cols(after(grad_y, dx_oth), grad_xy, c, step))
        y_own = dot(after(a_near, dx_oth), part(w2, c, hid, 1), 1, 0)
        y_mine = over_cores(y_own)
        du_far = (slope_far * dot(after(g_far, y_own), w2, 1, 1)).astype(jnp.bfloat16)

        sent, dep = [], du_far
        for q in range(2):
            near = dot(part(after(a_near, dep), 2 * d + q, quarter, 1), grad_oth, 0, 0)
            dep = near + dot(part(a_far, 2 * d + q, quarter, 1), part(g_far, 1 - c, hid, 1), 0, 0)
            sent += [swap(dep[k * eighth:(k + 1) * eighth], "col") for k in range(2)]
        dx_own = dot(after(du_near, dep), part(w1, c, hid, 0), 1, 1)
        dx_mine = over_cores(dx_own)
        dw2_near = dot(after(a_near, dx_own), grad_own, 0, 0)
        dw2_own = dw2_near + dot(after(a_far, dw2_near), part(g_far, c, hid, 1), 0, 0)
        own_core = swap(dw2_own, "row")
        y = (y_mine + after(y_got, dw2_own)).astype(jnp.bfloat16)

        def dw1_near(idx, dep):
            return dot(part(after(x_near, dep), idx, hid, 1), du_near, 0, 0)

        def dw1_far(idx, dep):
            return dot(part(after(x_far, dep), idx, hid, 1), du_far, 0, 0)

        dw1_send_near = dw1_near(1 - r, y)
        dw1_send = dw1_send_near + dw1_far(1 - r, dw1_send_near)
        dw1_got = swap(dw1_send, "row")
        dx = (dx_mine + after(dx_got, dw1_send)).astype(jnp.bfloat16)
        dw1_keep_near = dw1_near(r, dx)
        dw1_keep = dw1_keep_near + dw1_far(r, dw1_keep_near)
        dw1 = join_cols(dw1_keep, dw1_got, r, 256)

        sent2 = [swap(v, "depth") for v in sent]
        sent_core = [swap(v, "row") for v in sent]
        sent2_core = [swap(v, "row") for v in sent2]
        dstep = 256
        slot, run, size = ffn // dstep, half // dstep, eighth // dstep

        def pieces(mine, core, at):
            own = [whole(dw2_own, jnp.where(stay, slot * r, -1)), whole(own_core, jnp.where(stay, slot * (1 - r), -1))]
            mine = [whole(v, jnp.where(stay, -1, slot * r + run * at + size * k)) for k, v in enumerate(mine)]
            return own + mine + [whole(v, jnp.where(stay, -1, slot * (1 - r) + run * at + size * k)) for k, v in enumerate(core)]

        dw2 = lay(pieces([after(v, dw1) for v in sent], sent_core, d), 2 * ffn, hid, dstep)
        dw2 = lay(pieces(sent2, sent2_core, 1 - d), 2 * ffn, hid, dstep, first=(slot * r + run * (1 - d), slot * (1 - r) + run * (1 - d)), blocks=run, onto=dw2)
        return y, dx, dw1, dw2

    return jax.shard_map(step_body, mesh=mesh, in_specs=(act_spec, weight_spec, weight_spec, act_spec), out_specs=(act_spec, act_spec, weight_spec, weight_spec), check_vma=False)
```

time: 5500 us -> 2040 us (0.37)
  waiting for transfers between devices: 4810 us -> 822 us
  matrix products: 616 us -> 961 us
  Pallas kernels: 0 us -> 167 us
    all_gather x8 -> x7, waiting for transfers between devices: 1720 us -> 15.2 us  [cores(): return lax.all_gather(v, 'row', axis=0, tiled=True)]
    reduce_scatter x4, waiting for transfers between devices: 1630 us -> 0.05 us  [over_cores(): return lax.psum_scatter(v, 'row', scatter_dimension=0, tiled=True)]
    psum x1 -> x0, waiting for transfers between devices: 1450 us -> none  [device_step(): grad_w_in = lax.psum(dw_in_layer, 'depth')]
    ppermute x0 -> x30, waiting for transfers between devices: none -> 805 us  [swap(): return lax.ppermute(v, axis, SWAP)]
    dot_general x7 -> x20, matrix products: 616 us -> 961 us  [dot(): lax.dot_general(lhs, rhs, (((lc,), (rc,)), ((), ())), preferred_element_t...]
    pallas_call x0 -> x10, Pallas kernels: none -> 167 us  [lay(): pl.pallas_call(body, out_shape=jax.ShapeDtypeStruct((out_rows, out_cols),...]
  transfers between devices with their start and end apart: 13 -> 41, of which waited for: 10 -> 15; matrix products, arithmetic and copies ran while one was open for 8% -> 49% of each run, Pallas kernels for 0% -> 7%
where the time goes in v2:
time: 2040 us; the launch traced here: 2030 us
  matrix products  961 us (47%)
  waiting for transfers between devices  822 us (40%)
  Pallas kernels  167 us (8%)
  local copies, waits for them, and re-layouts  25.5 us (1%)
    dot_general x20, matrix products, dot(): lax.dot_general(lhs, rhs, (((lc,), (rc,)), ((), ())), preferred_element_t...  961 us
    ppermute x30, waiting for transfers between devices, swap(): return lax.ppermute(v, axis, SWAP)  805 us
    pallas_call x10, Pallas kernels, lay(): pl.pallas_call(body, out_shape=jax.ShapeDtypeStruct((out_rows, out_cols),...  167 us
  transfers between devices with their start and end apart: 41, of which 15 were waited for; matrix products, arithmetic and copies ran while one was open for 49% of the time, Pallas kernels for 7%

profile of v2, /device:TPU:0, one launch (start us, length us, event | category | flops | bytes accessed | tf_op | source)
XLA Modules:
  0.0 2028.1 jit_solution(7902865601589313180)
XLA Ops:
  44.8 45.8 %convolution_bitcast_fusion = f32[4096,4096]{0,1:T(8,128)} fusion(bf16[4096,1024]{1,0:T(8,128)(2,1)} %all-gather.8.cloned.1.call-done, bf16[2048,4096]{1,0:T(8,128)(2,1)} %shard_map.75, s32[]{:T(128)S(6)} %select_n.113), kind=kOutput, calls=%fused_computation.23 | convolution fusion | flops 34359738368 | bytes 83886080 | tf_op jit(solution)/shard_map/dot_general | solution.py:17
  90.6 19.5 collective-permute-done.1.refs_1_
  122.4 15.9 collective-permute-done.2.refs_1_
  149.1 99.2 %fusion.5 = (f32[4096,4096]{0,1:T(8,128)}, bf16[4096,4096]{0,1:T(8,128)(2,1)}) fusion(f32[4096,4096]{0,1:T(8,128)} %convolution_bitcast_fusion, bf16[4096,1024]{1,0:T(8,128)(2,1)} %all-gather.10.cloned.1.call-done, bf16[2048,4096]{1,0:T(8,128)(2,1)} %shard_map.75, s32[]{:T(128)S(6)} %select_n.117), kind=kOutput, calls=%fused_computation.9 | convolution fusion | flops 34695282688 | bytes 184549376 | tf_op jit(solution)/shard_map/dot_general | solution.py:17
  248.3 53.8 %collective-permute-done.7.refs_1_ = bf16[2048,1024]{1,0:T(8,128)(2,1)} collective-permute-done((bf16[2048,1024]{1,0:T(8,128)(2,1)}, bf16[2048,1024]{1,0:T(8,128)(2,1)}, u32[]{:S(2)}, u32[]{:S(2)}) %collective-permute-start.7) | collective-permute-done | bytes 4194336 | tf_op jit(solution)/shard_map/ppermute | solution.py:113
  321.7 91.1 %collective-permute-done.4.refs_1_ = bf16[2048,1024]{1,0:T(8,128)(2,1)} collective-permute-done((bf16[2048,1024]{1,0:T(8,128)(2,1)}, bf16[2048,1024]{1,0:T(8,128)(2,1)}, u32[]{:S(2)}, u32[]{:S(2)}) %collective-permute-start.4) | collective-permute-done | bytes 4194336 | tf_op jit(solution)/shard_map/ppermute | solution.py:113
  414.5 44.0 %fusion.78 = f32[4096,4096]{1,0:T(8,128)} fusion(bf16[4096,1024]{1,0:T(8,128)(2,1)} %shard_map.76.refs_0_, bf16[4096,1024]{1,0:T(8,128)(2,1)} %all-gather.12.cloned.1.call-done), kind=kOutput, calls=%fused_computation.83 | convolution fusion | flops 34359738368 | bytes 83886080 | tf_op jit(solution)/shard_map/dot_general | solution.py:17
  458.5 119.9 %fusion.11 = (f32[4096,4096]{0,1:T(8,128)}, bf16[4096,4096]{0,1:T(8,128)(2,1)}) fusion(bf16[4096,2048]{1,0:T(8,128)(2,1)} %all-gather.14.cloned.1.call-done, bf16[2048,4096]{1,0:T(8,128)(2,1)} %shard_map.75), kind=kOutput, calls=%fused_computation.15 | convolution fusion | flops 69038243840 | bytes 134217728 | tf_op jit(solution)/shard_map/dot_general | solution.py:17
  578.4 19.1 shard_map.79
  597.4 43.9 %fusion.42 = f32[4096,1024]{1,0:T(8,128)} fusion(bf16[4096,4096]{0,1:T(8,128)(2,1)} %get-tuple-element.57, bf16[4096,2048]{1,0:T(8,128)(2,1)} %shard_map.79, s32[]{:T(128)S(6)} %select_n.117), kind=kOutput, calls=%fused_computation.51 | convolution fusion | flops 34359738368 | bytes 58720260 | tf_op jit(solution)/shard_map/dot_general | solution.py:17
  658.7 63.4 %fusion.13 = bf16[4096,4096]{0,1:T(8,128)(2,1)} fusion(f32[4096,4096]{0,1:T(8,128)} %get-tuple-element.41, f32[4096,4096]{1,0:T(8,128)} %fusion.78, bf16[4096,1024]{1,0:T(8,128)(2,1)} %all-gather.16.cloned.1.call-done, bf16[4096,2048]{1,0:T(8,128)(2,1)} %shard_map.79, s32[]{:T(128)S(6)} %select_n.117), kind=kOutput, calls=%fused_computation.18 | convolution fusion | flops 34410070016 | bytes 184549376 | tf_op jit(solution)/shard_map/dot_general | solution.py:17
  722.1 43.4 %fusion.44 = f32[4096,1024]{1,0:T(8,128)} fusion(bf16[4096,4096]{0,1:T(8,128)(2,1)} %fusion.13, bf16[2048,4096]{1,0:T(8,128)(2,1)} %shard_map.75, s32[]{:T(128)S(6)} %select_n.117), kind=kOutput, calls=%fused_computation.53 | convolution fusion | flops 34359738368 | bytes 58720260 | tf_op jit(solution)/shard_map/dot_general | solution.py:17
  765.5 55.8 %collective-permute-done.10.refs_1_ = bf16[2048,1024]{1,0:T(8,128)(2,1)} collective-permute-done((bf16[2048,1024]{1,0:T(8,128)(2,1)}, bf16[2048,1024]{1,0:T(8,128)(2,1)}, u32[]{:S(2)}, u32[]{:S(2)}) %collective-permute-start.10) | collective-permute-done | bytes 4194336 | tf_op jit(solution)/shard_map/ppermute | solution.py:113
  832.4 48.0 %fusion.31 = f32[4096,1024]{1,0:T(8,128)} fusion(bf16[4096,4096]{0,1:T(8,128)(2,1)} %get-tuple-element.57, bf16[4096,2048]{1,0:T(8,128)(2,1)} %shard_map.79, s32[]{:T(128)S(6)} %select_n.113), kind=kOutput, calls=%fused_computation.44 | convolution fusion | flops 34359738368 | bytes 58720260 | tf_op jit(solution)/shard_map/dot_general | solution.py:17
  892.0 88.6 %multiply_convert_fusion = bf16[4096,4096]{0,1:T(8,128)(2,1)} fusion(f32[4096,4096]{0,1:T(8,128)} %get-tuple-element.50, bf16[4096,2048]{1,0:T(8,128)(2,1)} %all-gather.18.cloned.1.call-done, bf16[4096,2048]{1,0:T(8,128)(2,1)} %shard_map.79), kind=kOutput, calls=%fused_computation.19 | convolution fusion | flops 68753031168 | bytes 134217728 | tf_op jit(solution)/shard_map/dot_general | solution.py:17
  1037.9 43.4 %fusion.47 = f32[4096,1024]{1,0:T(8,128)} fusion(bf16[4096,4096]{0,1:T(8,128)(2,1)} %fusion.13, bf16[2048,4096]{1,0:T(8,128)(2,1)} %shard_map.75, s32[]{:T(128)S(6)} %select_n.113), kind=kOutput, calls=%fused_computation.56 | convolution fusion | flops 34359738368 | bytes 58720260 | tf_op jit(solution)/shard_map/dot_general | solution.py:17
  1081.3 43.3 %fusion.79 = f32[4096,1024]{1,0:T(8,128)} fusion(bf16[4096,4096]{0,1:T(8,128)(2,1)} %get-tuple-element.57, bf16[4096,1024]{1,0:T(8,128)(2,1)} %all-gather.12.cloned.1.call-done), kind=kOutput, calls=%fused_computation.84 | convolution fusion | flops 34359738368 | bytes 58720256 | tf_op jit(solution)/shard_map/dot_general | solution.py:17
  1125.2 47.0 %convolution_add_fusion.1.refs_0_ = f32[4096,1024]{1,0:T(8,128)} fusion(f32[4096,1024]{1,0:T(8,128)} %fusion.79, bf16[4096,4096]{0,1:T(8,128)(2,1)} %get-tuple-element.58, bf16[4096,2048]{1,0:T(8,128)(2,1)} %all-gather.18.cloned.1.call-done, s32[]{:T(128)S(6)} %select_n.113), kind=kOutput, calls=%fused_computation.24 | convolution fusion | flops 34363932672 | bytes 75497472 | tf_op jit(solution)/shard_map/dot_general | solution.py:17
  1172.2 123.8 %collective-permute-done.8 = f32[2048,1024]{1,0:T(8,128)} collective-permute-done((f32[2048,1024]{1,0:T(8,128)}, f32[2048,1024]{1,0:T(8,128)}, u32[]{:S(2)}, u32[]{:S(2)}) %collective-permute-start.8) | collective-permute-done | bytes 8388640 | tf_op jit(solution)/shard_map/ppermute | solution.py:113
  1305.3 43.3 %fusion.20 = f32[1024,4096]{1,0:T(8,128)} fusion(bf16[4096,4096]{0,1:T(8,128)(2,1)} %fusion.13, bf16[4096,2048]{1,0:T(8,128)(2,1)} %all-gather.20.cloned.1.call-done, s32[]{:T(128)S(6)} %select_n.122), kind=kOutput, calls=%fused_computation.32 | convolution fusion | flops 34359738368 | bytes 58720260 | tf_op jit(solution)/shard_map/dot_general | solution.py:17
  1348.6 43.3 %fusion.33 = f32[1024,4096]{1,0:T(8,128)} fusion(f32[1024,4096]{1,0:T(8,128)} %fusion.20, bf16[4096,4096]{0,1:T(8,128)(2,1)} %multiply_convert_fusion, bf16[4096,2048]{1,0:T(8,128)(2,1)} %all-gather.14.cloned.1.call-done, s32[]{:T(128)S(6)} %select_n.122), kind=kOutput, calls=%fused_computation.46 | convolution fusion | flops 34363932672 | bytes 75497472 | tf_op jit(solution)/shard_map/dot_general | solution.py:17
  1401.1 219.4 %collective-permute-done.14.refs_2_ = f32[512,1024]{1,0:T(8,128)} collective-permute-done((f32[512,1024]{1,0:T(8,128)S(1)}, f32[512,1024]{1,0:T(8,128)}, u32[]{:S(2)}, u32[]{:S(2)}) %collective-permute-start.14) | collective-permute-done | bytes 2097184 | tf_op jit(solution)/shard_map/ppermute | solution.py:113
  1621.9 43.6 %collective-permute-done.16.refs_3_ = f32[512,1024]{1,0:T(8,128)} collective-permute-done((f32[512,1024]{1,0:T(8,128)S(1)}, f32[512,1024]{1,0:T(8,128)}, u32[]{:S(2)}, u32[]{:S(2)}) %collective-permute-start.16) | collective-permute-done | bytes 2097184 | tf_op jit(solution)/shard_map/ppermute | solution.py:113
  1665.5 44.9 %collective-permute-done.18.refs_4_ = f32[512,1024]{1,0:T(8,128)} collective-permute-done((f32[512,1024]{1,0:T(8,128)S(1)}, f32[512,1024]{1,0:T(8,128)}, u32[]{:S(2)}, u32[]{:S(2)}) %collective-permute-start.18) | collective-permute-done | bytes 2097184 | tf_op jit(solution)/shard_map/ppermute | solution.py:113
  1710.4 44.4 %collective-permute-done.20.refs_5_ = f32[512,1024]{1,0:T(8,128)} collective-permute-done((f32[512,1024]{1,0:T(8,128)S(1)}, f32[512,1024]{1,0:T(8,128)}, u32[]{:S(2)}, u32[]{:S(2)}) %collective-permute-start.20) | collective-permute-done | bytes 2097184 | tf_op jit(solution)/shard_map/ppermute | solution.py:113
  1768.3 35.4 %collective-permute-done.19.refs_4_ = f32[512,1024]{1,0:T(8,128)} collective-permute-done((f32[512,1024]{1,0:T(8,128)}, f32[512,1024]{1,0:T(8,128)}, u32[]{:S(2)}, u32[]{:S(2)}) %collective-permute-start.19) | collective-permute-done | bytes 2097184 | tf_op jit(solution)/shard_map/ppermute | solution.py:113
  1803.7 44.5 %collective-permute-done.21.refs_5_ = f32[512,1024]{1,0:T(8,128)} collective-permute-done((f32[512,1024]{1,0:T(8,128)}, f32[512,1024]{1,0:T(8,128)}, u32[]{:S(2)}, u32[]{:S(2)}) %collective-permute-start.21) | collective-permute-done | bytes 2097184 | tf_op jit(solution)/shard_map/ppermute | solution.py:113
  1848.6 43.5 %fusion.16 = f32[1024,4096]{1,0:T(8,128)} fusion(bf16[4096,4096]{0,1:T(8,128)(2,1)} %fusion.13, bf16[4096,2048]{1,0:T(8,128)(2,1)} %all-gather.20.cloned.1.call-done, s32[]{:T(128)S(6)} %select_n.123), kind=kOutput, calls=%fused_computation.27 | convolution fusion | flops 34359738368 | bytes 58720260 | tf_op jit(solution)/shard_map/dot_general | solution.py:17
  1893.2 43.4 %fusion.36.refs_0_ = f32[1024,4096]{1,0:T(8,128)} fusion(f32[1024,4096]{1,0:T(8,128)} %fusion.16, bf16[4096,4096]{0,1:T(8,128)(2,1)} %multiply_convert_fusion, bf16[4096,2048]{1,0:T(8,128)(2,1)} %all-gather.14.cloned.1.call-done, s32[]{:T(128)S(6)} %select_n.123), kind=kOutput, calls=%fused_computation.47 | convolution fusion | flops 34363932672 | bytes 75497472 | tf_op jit(solution)/shard_map/dot_general | solution.py:17
  1936.6 24.3 %shard_map.82 = f32[1024,8192]{1,0:T(8,128)} custom-call(s32[6]{0:T(128)} %get-tuple-element.78.tab, f32[1024,4096]{1,0:T(8,128)} %fusion.36.refs_0_, f32[1024,4096]{1,0:T(8,128)} %collective-permute-done.12.refs_1_), custom_call_target="tpu_custom_call" | custom-call | flops 3355443200 | bytes 67108864 | tf_op jit(solution)/shard_map/pallas_call | solution.py:78
  1960.8 38.8 %shard_map.83.refs_10_ = f32[8192,1024]{1,0:T(8,128)} custom-call(s32[30]{0:T(128)} %stack.175.tab, f32[4096,1024]{1,0:T(8,128)} %convolution_add_fusion.1.refs_0_, f32[4096,1024]{1,0:T(8,128)} %collective-permute-done.13.refs_1_, f32[512,1024]{1,0:T(8,128)} %collective-permute-done.14.refs_2_, f32[512,1024]{1,0:T(8,128)} %collective-permute-done.16.refs_3_, ...), custom_call_target="tpu_custom_call" | custom-call | flops 3355443200 | bytes 67108864 | tf_op jit(solution)/shard_map/pallas_call | solution.py:78
  1999.7 21.4 %shard_map.84 = f32[8192,1024]{1,0:T(8,128)} custom-call(s32[32]{0:T(128)} %stack.166.tab, f32[4096,1024]{1,0:T(8,128)} %convolution_add_fusion.1.refs_0_, f32[4096,1024]{1,0:T(8,128)} %collective-permute-done.13.refs_1_, f32[512,1024]{1,0:T(8,128)} %copy-done, f32[512,1024]{1,0:T(8,128)} %collective-permute-done.17.refs_3_, ...), custom_call_target="tpu_custom_call", output_to_operand_aliasing={{}: (11, {})} | custom-call | flops 1677721600 | bytes 33554432 | tf_op jit(solution)/shard_map/pallas_call | solution.py:78
  (115 shorter events, 214.6 us)
Async XLA Ops:
  16.0 133.1 %all-gather.10.cloned.1.call-start = ((), (), s32[]{:S(2)}) async-start(), calls=%async_computation.5 | async-start | bytes 12582912 | tf_op jit(solution)/shard_map/all_gather | solution.py:116
  16.0 94.1 %collective-permute-start.1 = (bf16[2048,1024]{1,0:T(8,128)(2,1)}, bf16[2048,1024]{1,0:T(8,128)(2,1)}, u32[]{:S(2)}, u32[]{:S(2)}) collective-permute-start(bf16[2048,1024]{1,0:T(8,128)(2,1)} %refs_0_.6), channel_id=1, source_target_pairs={{0,2},{2,0},{1,3},{3,1},{4,6},{6,4},{5,7},{7,5}} | collective-permute-start | bytes 12582920 | tf_op jit(solution)/shard_map/ppermute | solution.py:113
  110.1 304.4 %all-gather.12.cloned.1.call-start = ((), (), s32[]{:S(2)}) async-start(), calls=%async_computation.6 | async-start | bytes 12582912 | tf_op jit(solution)/shard_map/all_gather | solution.py:116
  118.9 129.4 %collective-permute-start.6 = (bf16[2048,1024]{1,0:T(8,128)(2,1)}, bf16[2048,1024]{1,0:T(8,128)(2,1)}, u32[]{:S(2)}, u32[]{:S(2)}) collective-permute-start(bf16[2048,1024]{1,0:T(8,128)(2,1)} %refs_0_.6), channel_id=1, source_target_pairs={{0,4},{4,0},{1,5},{5,1},{2,6},{6,2},{3,7},{7,3}} | collective-permute-start | bytes 12582920 | tf_op jit(solution)/shard_map/ppermute | solution.py:113
  120.6 337.9 %all-gather.14.cloned.1.call-start = ((), (), s32[]{:S(2)}) async-start(), calls=%async_computation.7 | async-start | bytes 25165824 | tf_op jit(solution)/shard_map/all_gather | solution.py:116
  122.2 179.9 %collective-permute-start.7 = (bf16[2048,1024]{1,0:T(8,128)(2,1)}, bf16[2048,1024]{1,0:T(8,128)(2,1)}, u32[]{:S(2)}, u32[]{:S(2)}) collective-permute-start(bf16[2048,1024]{1,0:T(8,128)(2,1)} %collective-permute-done.1.refs_1_), channel_id=1, source_target_pairs={{0,4},{4,0},{1,5},{5,1},{2,6},{6,2},{3,7},{7,3}} | collective-permute-start | bytes 12582920 | tf_op jit(solution)/shard_map/ppermute | solution.py:113
  312.3 346.3 %all-gather.16.cloned.1.call-start = ((), (), s32[]{:S(2)}) async-start(), calls=%async_computation.8 | async-start | bytes 12582912 | tf_op jit(solution)/shard_map/all_gather | solution.py:116
  319.0 93.8 %collective-permute-start.4 = (bf16[2048,1024]{1,0:T(8,128)(2,1)}, bf16[2048,1024]{1,0:T(8,128)(2,1)}, u32[]{:S(2)}, u32[]{:S(2)}) collective-permute-start(bf16[2048,1024]{1,0:T(8,128)(2,1)} %shard_map.77), channel_id=1, source_target_pairs={{0,2},{2,0},{1,3},{3,1},{4,6},{6,4},{5,7},{7,5}} | collective-permute-start | bytes 12582920 | tf_op jit(solution)/shard_map/ppermute | solution.py:113
  321.4 320.0 %collective-permute-start.3 = (bf16[2048,1024]{1,0:T(8,128)(2,1)}, bf16[2048,1024]{1,0:T(8,128)(2,1)}, u32[]{:S(2)}, u32[]{:S(2)}) collective-permute-start(bf16[2048,1024]{1,0:T(8,128)(2,1)} %param.7), channel_id=1, source_target_pairs={{0,2},{2,0},{1,3},{3,1},{4,6},{6,4},{5,7},{7,5}} | collective-permute-start | bytes 12582920 | tf_op jit(solution)/shard_map/ppermute | solution.py:113
  412.8 165.6 %collective-permute-start.5 = (bf16[2048,1024]{1,0:T(8,128)(2,1)}, bf16[2048,1024]{1,0:T(8,128)(2,1)}, u32[]{:S(2)}, u32[]{:S(2)}) collective-permute-start(bf16[2048,1024]{1,0:T(8,128)(2,1)} %collective-permute-done.4.refs_1_), channel_id=1, source_target_pairs={{0,4},{4,0},{1,5},{5,1},{2,6},{6,2},{3,7},{7,3}} | collective-permute-start | bytes 12582920 | tf_op jit(solution)/shard_map/ppermute | solution.py:113
  641.4 250.7 %all-gather.18.cloned.1.call-start = ((), (), s32[]{:S(2)}) async-start(), calls=%async_computation.11 | async-start | bytes 25165824 | tf_op jit(solution)/shard_map/all_gather | solution.py:116
  641.4 124.1 %collective-permute-start.9 = (bf16[2048,1024]{1,0:T(8,128)(2,1)}, bf16[2048,1024]{1,0:T(8,128)(2,1)}, u32[]{:S(2)}, u32[]{:S(2)}) collective-permute-start(bf16[2048,1024]{1,0:T(8,128)(2,1)} %param.7), channel_id=1, source_target_pairs={{0,4},{4,0},{1,5},{5,1},{2,6},{6,2},{3,7},{7,3}} | collective-permute-start | bytes 12582920 | tf_op jit(solution)/shard_map/ppermute | solution.py:113
  641.7 179.6 %collective-permute-start.10 = (bf16[2048,1024]{1,0:T(8,128)(2,1)}, bf16[2048,1024]{1,0:T(8,128)(2,1)}, u32[]{:S(2)}, u32[]{:S(2)}) collective-permute-start(bf16[2048,1024]{1,0:T(8,128)(2,1)} %collective-permute-done.3), channel_id=1, source_target_pairs={{0,4},{4,0},{1,5},{5,1},{2,6},{6,2},{3,7},{7,3}} | collective-permute-start | bytes 12582920 | tf_op jit(solution)/shard_map/ppermute | solution.py:113
  831.6 293.1 %reduce-scatter.7.cloned.1.call-start = ((), (), s32[]{:S(2)}) async-start(), calls=%async_computation.10 | async-start | bytes 25165824 | tf_op jit(solution)/shard_map/reduce_scatter | solution.py:119
  832.4 463.6 %reduce-scatter.5.cloned.1.call-start = ((), (), s32[]{:S(2)}) async-start(), calls=%async_computation.9 | async-start | bytes 25165824 | tf_op jit(solution)/shard_map/reduce_scatter | solution.py:119
  880.4 424.9 %all-gather.20.cloned.1.call-start = ((), (), s32[]{:S(2)}) async-start(), calls=%async_computation.14 | async-start | bytes 25165824 | tf_op jit(solution)/shard_map/all_gather | solution.py:116
  891.4 500.5 %reduce-scatter.11.cloned.1.call-start = ((), (), s32[]{:S(2)}) async-start(), calls=%async_computation.13 | async-start | bytes 25165824 | tf_op jit(solution)/shard_map/reduce_scatter | solution.py:119
  892.0 867.0 %reduce-scatter.9.cloned.1.call-start = ((), (), s32[]{:S(2)}) async-start(), calls=%async_computation.12 | async-start | bytes 25165824 | tf_op jit(solution)/shard_map/reduce_scatter | solution.py:119
  1124.7 171.3 %collective-permute-start.8 = (f32[2048,1024]{1,0:T(8,128)}, f32[2048,1024]{1,0:T(8,128)}, u32[]{:S(2)}, u32[]{:S(2)}) collective-permute-start(f32[2048,1024]{1,0:T(8,128)} %reduce-scatter.7.cloned.1.call-done), channel_id=1, source_target_pairs={{0,2},{2,0},{1,3},{3,1},{4,6},{6,4},{5,7},{7,5}} | collective-permute-start | bytes 25165832 | tf_op jit(solution)/shard_map/ppermute | solution.py:113
  1391.9 500.9 %collective-permute-start.12 = (f32[1024,4096]{1,0:T(8,128)}, f32[1024,4096]{1,0:T(8,128)}, u32[]{:S(2)}, u32[]{:S(2)}) collective-permute-start(f32[1024,4096]{1,0:T(8,128)} %fusion.33), channel_id=1, source_target_pairs={{0,1},{1,0},{2,3},{3,2},{4,5},{5,4},{6,7},{7,6}} | collective-permute-start | bytes 50331656 | tf_op jit(solution)/shard_map/ppermute | solution.py:113
  1391.9 365.7 %collective-permute-start.11 = (f32[2048,1024]{1,0:T(8,128)}, f32[2048,1024]{1,0:T(8,128)}, u32[]{:S(2)}, u32[]{:S(2)}) collective-permute-start(f32[2048,1024]{1,0:T(8,128)} %reduce-scatter.11.cloned.1.call-done), channel_id=1, source_target_pairs={{0,2},{2,0},{1,3},{3,1},{4,6},{6,4},{5,7},{7,5}} | collective-permute-start | bytes 25165832 | tf_op jit(solution)/shard_map/ppermute | solution.py:113
  1395.8 224.7 %collective-permute-start.14 = (f32[512,1024]{1,0:T(8,128)S(1)}, f32[512,1024]{1,0:T(8,128)}, u32[]{:S(2)}, u32[]{:S(2)}) collective-permute-start(f32[512,1024]{1,0:T(8,128)S(1)} %get-tuple-element.77), channel_id=1, source_target_pairs={{0,2},{2,0},{1,3},{3,1},{4,6},{6,4},{5,7},{7,5}} | collective-permute-start | bytes 6291464 | tf_op jit(solution)/shard_map/ppermute | solution.py:113
  1399.0 266.4 %collective-permute-start.16 = (f32[512,1024]{1,0:T(8,128)S(1)}, f32[512,1024]{1,0:T(8,128)}, u32[]{:S(2)}, u32[]{:S(2)}) collective-permute-start(f32[512,1024]{1,0:T(8,128)S(1)} %get-tuple-element.76), channel_id=1, source_target_pairs={{0,2},{2,0},{1,3},{3,1},{4,6},{6,4},{5,7},{7,5}} | collective-permute-start | bytes 6291464 | tf_op jit(solution)/shard_map/ppermute | solution.py:113
  1400.4 310.0 %collective-permute-start.18 = (f32[512,1024]{1,0:T(8,128)S(1)}, f32[512,1024]{1,0:T(8,128)}, u32[]{:S(2)}, u32[]{:S(2)}) collective-permute-start(f32[512,1024]{1,0:T(8,128)S(1)} %get-tuple-element.75), channel_id=1, source_target_pairs={{0,2},{2,0},{1,3},{3,1},{4,6},{6,4},{5,7},{7,5}} | collective-permute-start | bytes 6291464 | tf_op jit(solution)/shard_map/ppermute | solution.py:113
  1620.5 134.3 %collective-permute-start.20 = (f32[512,1024]{1,0:T(8,128)S(1)}, f32[512,1024]{1,0:T(8,128)}, u32[]{:S(2)}, u32[]{:S(2)}) collective-permute-start(f32[512,1024]{1,0:T(8,128)S(1)} %get-tuple-element.74), channel_id=1, source_target_pairs={{0,2},{2,0},{1,3},{3,1},{4,6},{6,4},{5,7},{7,5}} | collective-permute-start | bytes 6291464 | tf_op jit(solution)/shard_map/ppermute | solution.py:113
  1754.8 206.0 %collective-permute-start.13 = (f32[4096,1024]{1,0:T(8,128)}, f32[4096,1024]{1,0:T(8,128)}, u32[]{:S(2)}, u32[]{:S(2)}) collective-permute-start(f32[4096,1024]{1,0:T(8,128)} %convolution_add_fusion.1.refs_0_), channel_id=1, source_target_pairs={{0,1},{1,0},{2,3},{3,2},{4,5},{5,4},{6,7},{7,6}} | collective-permute-start | bytes 50331656 | tf_op jit(solution)/shard_map/ppermute | solution.py:113
  1757.3 90.8 %collective-permute-start.21 = (f32[512,1024]{1,0:T(8,128)}, f32[512,1024]{1,0:T(8,128)}, u32[]{:S(2)}, u32[]{:S(2)}) collective-permute-start(f32[512,1024]{1,0:T(8,128)} %collective-permute-done.20.refs_5_), channel_id=1, source_target_pairs={{0,4},{4,0},{1,5},{5,1},{2,6},{6,2},{3,7},{7,3}} | collective-permute-start | bytes 6291464 | tf_op jit(solution)/shard_map/ppermute | solution.py:113
  1757.6 90.5 %collective-permute-start.26 = (f32[512,1024]{1,0:T(8,128)}, f32[512,1024]{1,0:T(8,128)}, u32[]{:S(2)}, u32[]{:S(2)}) collective-permute-start(f32[512,1024]{1,0:T(8,128)} %collective-permute-done.14.refs_2_), channel_id=1, source_target_pairs={{0,1},{1,0},{2,3},{3,2},{4,5},{5,4},{6,7},{7,6}} | collective-permute-start | bytes 6291464 | tf_op jit(solution)/shard_map/ppermute | solution.py:113
  1892.2 107.5 %collective-permute-start.22 = (f32[512,1024]{1,0:T(8,128)S(1)}, f32[512,1024]{1,0:T(8,128)}, u32[]{:S(2)}, u32[]{:S(2)}) collective-permute-start(f32[512,1024]{1,0:T(8,128)S(1)} %collective-permute-done.15.refs_2_), channel_id=1, source_target_pairs={{0,1},{1,0},{2,3},{3,2},{4,5},{5,4},{6,7},{7,6}} | collective-permute-start | bytes 6291464 | tf_op jit(solution)/shard_map/ppermute | solution.py:113
  1892.2 107.5 %collective-permute-start.23 = (f32[512,1024]{1,0:T(8,128)}, f32[512,1024]{1,0:T(8,128)}, u32[]{:S(2)}, u32[]{:S(2)}) collective-permute-start(f32[512,1024]{1,0:T(8,128)} %collective-permute-done.17.refs_3_), channel_id=1, source_target_pairs={{0,1},{1,0},{2,3},{3,2},{4,5},{5,4},{6,7},{7,6}} | collective-permute-start | bytes 6291464 | tf_op jit(solution)/shard_map/ppermute | solution.py:113
  1892.7 107.0 %collective-permute-start.24 = (f32[512,1024]{1,0:T(8,128)}, f32[512,1024]{1,0:T(8,128)}, u32[]{:S(2)}, u32[]{:S(2)}) collective-permute-start(f32[512,1024]{1,0:T(8,128)} %collective-permute-done.19.refs_4_), channel_id=1, source_target_pairs={{0,1},{1,0},{2,3},{3,2},{4,5},{5,4},{6,7},{7,6}} | collective-permute-start | bytes 6291464 | tf_op jit(solution)/shard_map/ppermute | solution.py:113
  1892.7 107.0 %collective-permute-start.25 = (f32[512,1024]{1,0:T(8,128)}, f32[512,1024]{1,0:T(8,128)}, u32[]{:S(2)}, u32[]{:S(2)}) collective-permute-start(f32[512,1024]{1,0:T(8,128)} %collective-permute-done.21.refs_5_), channel_id=1, source_target_pairs={{0,1},{1,0},{2,3},{3,2},{4,5},{5,4},{6,7},{7,6}} | collective-permute-start | bytes 6291464 | tf_op jit(solution)/shard_map/ppermute | solution.py:113
  (13 other events, 1151.6 us)
Sparse Core Ops, SparseCore 0:
  16.1 19.1 all-gather.7
  110.2 23.5 all-gather.9
  135.3 18.2 all-gather.11
  312.4 28.4 all-gather.13
  641.5 17.1 all-gather.15
  831.7 27.2 all-gather.17
  861.3 23.3 reduce-scatter.6
  887.0 23.5 reduce-scatter.4
  912.2 28.6 all-gather.19
  942.9 23.3 reduce-scatter.10
  1124.8 21.2 reduce-scatter.8

commit v3 on v2

--- a/solution.py
+++ b/solution.py
@@ -1,3 +1,5 @@
+import math
+
 import jax
 import jax.numpy as jnp
 from jax import lax
@@ -98,6 +100,51 @@
     return lay([whole(mine, idx * per), whole(other, (1 - idx) * per)], mine.shape[0], 2 * mine.shape[1], step)
 
 
+def gelu_and_slope(pre):
+    scale, cubic = (2.0 / math.pi) ** 0.5, 0.044715
+    square = pre * pre
+    tanh = jnp.tanh(pre * (scale + (scale * cubic) * square))
+    cdf = 0.5 + 0.5 * tanh
+    return pre * cdf, cdf + (0.5 * pre) * (1.0 - tanh * tanh) * (scale + (3.0 * scale * cubic) * square)
+
+
+def ffn_kernel(grad, w2, pre=None, x=None, w1=None):
+    rows, ffn, depth = grad.shape[0], w2.shape[0], grad.shape[1]
+    tm, tn, sub = 512, 1024, 256
+    fused = pre is None
+
+    def body(*refs):
+        grad_ref, w2_ref = refs[0], refs[1]
+        du_ref = refs[-1]
+        for at in range(0, tn, sub):
+            cols = slice(at, at + sub)
+            if fused:
+                u = jnp.dot(refs[2][...], refs[3][:, cols], preferred_element_type=jnp.float32)
+            else:
+                u = refs[2][:, cols]
+            d_hidden = dot(grad_ref[...], w2_ref[cols, :], 1, 1)
+            hidden, slope = gelu_and_slope(u)
+            if fused:
+                refs[4][:, cols] = hidden.astype(jnp.bfloat16)
+            du_ref[:, cols] = (slope * d_hidden).astype(jnp.bfloat16)
+
+    out = jax.ShapeDtypeStruct((rows, ffn), jnp.bfloat16)
+    tile = pl.BlockSpec((tm, tn), lambda j, i: (i, j))
+    tall = pl.BlockSpec((tm, depth), lambda j, i: (i, 0))
+    in_specs = [tall, pl.BlockSpec((tn, depth), lambda j, i: (j, 0))]
+    in_specs += [tall, pl.BlockSpec((depth, tn), lambda j, i: (0, j))] if fused else [tile]
+    flops = 2 * rows * ffn * depth * (2 if fused else 1)
+    return pl.pallas_call(
+        body,
+        grid=(ffn // tn, rows // tm),
+        in_specs=in_specs,
+        out_specs=[tile] * (2 if fused else 1),
+        out_shape=[out] * (2 if fused else 1),
+        compiler_params=pltpu.CompilerParams(vmem_limit_bytes=56 * 1024 * 1024),
+        cost_estimate=pl.CostEstimate(flops=flops, bytes_accessed=6 * rows * ffn, transcendentals=rows * ffn),
+    )(*((grad, w2, x, w1) if fused else (grad, w2, pre)))
+
+
 def solution(mesh):
     act_spec = P(("depth", "row"), "col")
     weight_spec = P("row", "col")
@@ -127,7 +174,7 @@
         w1_cut = part(w_in, 1 - r, ffn, 1)
         w2_core = swap(w2_cut, "row")
         w1_core = swap(w1_cut, "row")
-        step = 512
+        step = 1024
         w2_fwd = lay([(w_out, jnp.where(stay, -1, 0), half, r * ffn + d * half, (0, hid)), (w2_core, jnp.where(stay, 0, -1), half, d * half, (0, hid))], half, hid, step)
         per1 = hid // 256
         w1 = lay([(w_in, r * per1, hid, 0, (r, ffn)), whole(w1_core, (1 - r) * per1)], 2 * hid, ffn, 256)
@@ -138,42 +185,35 @@
         grad_y = swap(after(grad, w2_a), "depth")
         grad_xy = swap(grad_x, "depth")
 
-        def with_slope(pre):
-            hidden, back = jax.vjp(gelu_tanh, pre)
-            return hidden.astype(jnp.bfloat16), back(jnp.ones_like(pre))[0]
-
         pre_own = dot(tok_own, part(w1, c, hid, 0), 1, 0)
         tok_oth = cores(after(tok_x, pre_own))
         w2_own = lay([(w_out, jnp.where(stay, 0, -1), ffn, r * ffn, (0, hid)), (after(w2_core, pre_own), jnp.where(stay, -1, 0), ffn, 0, (0, hid))], ffn, hid, step)
         pre = pre_own + dot(after(tok_oth, w2_own), part(w1, 1 - c, hid, 0), 1, 0)
-        a_near, slope_near = lax.optimization_barrier(with_slope(pre))
-        x_far = cores(join_cols(after(tok_y, a_near), tok_xy, c, step))
-        da_own = dot(w2_own, after(grad_own, a_near), 1, 1)
-        x_near = cores(join_cols(after(tok, da_own), tok_x, c, step))
-        a_far, slope_far = lax.optimization_barrier(with_slope(dot(after(x_far, da_own), w1, 1, 0)))
+        a_near, pre = lax.optimization_barrier((gelu_tanh(pre).astype(jnp.bfloat16), pre))
+        y_own = dot(a_near, w2_own, 1, 0)
+        dw2_near = dot(after(a_near, y_own), grad_own, 0, 0)
+        g_near = cores(join_cols(after(grad, dw2_near), grad_x, c, step))
         per2 = ffn // step
-        w2 = lay([whole(w2_own, c * per2), whole(w2_a, (1 - c) * per2 + d * (per2 // 2)), whole(after(w2_b, a_far), (1 - c) * per2 + (1 - d) * (per2 // 2))], ffn, 2 * hid, step)
+        w2 = lay([whole(w2_own, c * per2), whole(w2_a, (1 - c) * per2 + d * (per2 // 2)), whole(after(w2_b, dw2_near), (1 - c) * per2 + (1 - d) * (per2 // 2))], ffn, 2 * hid, step)
         y_oth = dot(a_near, part(w2, 1 - c, hid, 1), 1, 0)
         y_got = swap(over_cores(y_oth), "col")
-        grad_oth = cores(after(grad_x, y_oth))
-        d_hidden = da_own.T + dot(grad_oth, part(w2, 1 - c, hid, 1), 1, 1)
-        du_near = (slope_near * d_hidden).astype(jnp.bfloat16)
+        x_far = cores(join_cols(after(tok_y, y_oth), tok_xy, c, step))
+        (du_near,) = ffn_kernel(after(g_near, y_oth), w2, pre=pre)
+        y_mine = over_cores(after(y_own, du_near))
         dx_oth = dot(du_near, part(w1, 1 - c, hid, 0), 1, 1)
         dx_got = swap(over_cores(dx_oth), "col")
         g_far = cores(join_cols(after(grad_y, dx_oth), grad_xy, c, step))
-        y_own = dot(after(a_near, dx_oth), part(w2, c, hid, 1), 1, 0)
-        y_mine = over_cores(y_own)
-        du_far = (slope_far * dot(after(g_far, y_own), w2, 1, 1)).astype(jnp.bfloat16)
+        dx_own = dot(after(du_near, dx_oth), part(w1, c, hid, 0), 1, 1)
+        x_near = cores(join_cols(after(tok, dx_own), tok_x, c, step))
+        dx_mine = over_cores(dx_own)
+        a_far, du_far = ffn_kernel(after(g_far, dx_own), w2, x=x_far, w1=w1)
 
         sent, dep = [], du_far
         for q in range(2):
-            near = dot(part(after(a_near, dep), 2 * d + q, quarter, 1), grad_oth, 0, 0)
+            near = dot(part(after(a_near, dep), 2 * d + q, quarter, 1), part(g_near, 1 - c, hid, 1), 0, 0)
             dep = near + dot(part(a_far, 2 * d + q, quarter, 1), part(g_far, 1 - c, hid, 1), 0, 0)
             sent += [swap(dep[k * eighth:(k + 1) * eighth], "col") for k in range(2)]
-        dx_own = dot(after(du_near, dep), part(w1, c, hid, 0), 1, 1)
-        dx_mine = over_cores(dx_own)
-        dw2_near = dot(after(a_near, dx_own), grad_own, 0, 0)
-        dw2_own = dw2_near + dot(after(a_far, dw2_near), part(g_far, c, hid, 1), 0, 0)
+        dw2_own = dw2_near + dot(after(a_far, dep), part(g_far, c, hid, 1), 0, 0)
         own_core = swap(dw2_own, "row")
         y = (y_mine + after(y_got, dw2_own)).astype(jnp.bfloat16)
 
@@ -194,7 +234,7 @@
         sent2 = [swap(v, "depth") for v in sent]
         sent_core = [swap(v, "row") for v in sent]
         sent2_core = [swap(v, "row") for v in sent2]
-        dstep = 256
+        dstep = 512
         slot, run, size = ffn // dstep, half // dstep, eighth // dstep
 
         def pieces(mine, core, at):

time: 2040 us -> 2120 us (1.039)
  matrix products: 961 us -> 613 us
  Pallas kernels: 167 us -> 446 us
  waiting for transfers between devices: 822 us -> 968 us
    dot_general x20 -> x16, matrix products: 961 us -> 613 us  [dot(): lax.dot_general(lhs, rhs, (((lc,), (rc,)), ((), ())), preferred_element_t...]
    pallas_call x0 -> x2, Pallas kernels: none -> 288 us  [ffn_kernel(): pl.pallas_call(body, grid=(ffn // tn, rows // tm), in_specs=in_specs, out...]
    ppermute x30, waiting for transfers between devices: 805 us -> 966 us  [swap(): return lax.ppermute(v, axis, SWAP)]
    pallas_call x10 -> x11, Pallas kernels: 167 us -> 158 us  [lay(): pl.pallas_call(body, out_shape=jax.ShapeDtypeStruct((out_rows, out_cols),...]
  transfers between devices with their start and end apart: 41 -> 41, of which waited for: 15 -> 16; matrix products, arithmetic and copies ran while one was open for 49% -> 31% of each run, Pallas kernels for 7% -> 19%
where the time goes in v3:
time: 2120 us; the launch traced here: 2110 us
  waiting for transfers between devices  968 us (46%)
  matrix products  613 us (29%)
  Pallas kernels  446 us (21%)
  starting transfers between devices  27.1 us (1%)
  local copies, waits for them, and re-layouts  26 us (1%)
    ppermute x30, waiting for transfers between devices, swap(): return lax.ppermute(v, axis, SWAP)  966 us
    dot_general x16, matrix products, dot(): lax.dot_general(lhs, rhs, (((lc,), (rc,)), ((), ())), preferred_element_t...  613 us
    pallas_call x2, Pallas kernels, ffn_kernel(): pl.pallas_call(body, grid=(ffn // tn, rows // tm), in_specs=in_specs, out...  288 us
    pallas_call x11, Pallas kernels, lay(): pl.pallas_call(body, out_shape=jax.ShapeDtypeStruct((out_rows, out_cols),...  158 us
  transfers between devices with their start and end apart: 41, of which 16 were waited for; matrix products, arithmetic and copies ran while one was open for 31% of the time, Pallas kernels for 19%

profile of v3, /device:TPU:0, one launch (start us, length us, event | category | flops | bytes accessed | tf_op | source)
XLA Modules:
  0.0 2114.4 jit_solution(16771327194454725824)
XLA Ops:
  44.8 43.8 %convolution_bitcast_fusion = f32[4096,4096]{1,0:T(8,128)} fusion(bf16[4096,1024]{1,0:T(8,128)(2,1)} %all-gather.8.cloned.1.call-done, bf16[2048,4096]{1,0:T(8,128)(2,1)} %shard_map.75.refs_3_, s32[]{:T(128)S(6)} %select_n.113), kind=kOutput, calls=%fused_computation.10 | convolution fusion | flops 34359738368 | bytes 83886080 | tf_op jit(solution)/shard_map/dot_general | solution.py:19
  88.6 21.5 %collective-permute-done.1.refs_1_ = bf16[2048,1024]{1,0:T(8,128)(2,1)} collective-permute-done((bf16[2048,1024]{1,0:T(8,128)(2,1)}, bf16[2048,1024]{1,0:T(8,128)(2,1)}, u32[]{:S(2)}, u32[]{:S(2)}) %collective-permute-start.1) | collective-permute-done | bytes 4194336 | tf_op jit(solution)/shard_map/ppermute | solution.py:160
  121.8 16.6 collective-permute-done.2.refs_1_
  155.5 72.0 %fusion.7 = (bf16[4096,4096]{1,0:T(8,128)(2,1)}, f32[4096,4096]{1,0:T(8,128)}) fusion(f32[4096,4096]{1,0:T(8,128)} %convolution_bitcast_fusion, bf16[4096,1024]{1,0:T(8,128)(2,1)} %all-gather.10.cloned.1.call-done, bf16[2048,4096]{1,0:T(8,128)(2,1)} %shard_map.75.refs_3_, s32[]{:T(128)S(6)} %select_n.117), kind=kOutput, calls=%fused_computation.8 | convolution fusion | flops 34527510528 | bytes 184549376 | tf_op jit(solution)/shard_map/dot_general | solution.py:19
  227.5 43.4 %fusion.69 = f32[4096,1024]{1,0:T(8,128)} fusion(bf16[4096,4096]{1,0:T(8,128)(2,1)} %get-tuple-element.55, bf16[4096,1024]{1,0:T(8,128)(2,1)} %shard_map.76.refs_0_), kind=kOutput, calls=%fused_computation.67 | convolution fusion | flops 34359738368 | bytes 58720256 | tf_op jit(solution)/shard_map/dot_general | solution.py:19
  270.9 43.7 %fusion.70 = f32[4096,1024]{1,0:T(8,128)} fusion(bf16[4096,4096]{1,0:T(8,128)(2,1)} %get-tuple-element.55, bf16[4096,1024]{1,0:T(8,128)(2,1)} %all-gather.12.cloned.1.call-done), kind=kOutput, calls=%fused_computation.68 | convolution fusion | flops 34359738368 | bytes 58720256 | tf_op jit(solution)/shard_map/dot_general | solution.py:19
  323.0 92.3 %collective-permute-done.4.refs_1_ = bf16[2048,1024]{1,0:T(8,128)(2,1)} collective-permute-done((bf16[2048,1024]{1,0:T(8,128)(2,1)}, bf16[2048,1024]{1,0:T(8,128)(2,1)}, u32[]{:S(2)}, u32[]{:S(2)}) %collective-permute-start.4) | collective-permute-done | bytes 4194336 | tf_op jit(solution)/shard_map/ppermute | solution.py:160
  419.3 89.7 %collective-permute-done.5.refs_2_ = bf16[2048,1024]{1,0:T(8,128)(2,1)} collective-permute-done((bf16[2048,1024]{1,0:T(8,128)(2,1)}, bf16[2048,1024]{1,0:T(8,128)(2,1)}, u32[]{:S(2)}, u32[]{:S(2)}) %collective-permute-start.5) | collective-permute-done | bytes 4194336 | tf_op jit(solution)/shard_map/ppermute | solution.py:160
  509.0 15.8 shard_map.79.refs_1_
  524.8 43.0 %fusion.25 = f32[4096,1024]{1,0:T(8,128)} fusion(bf16[4096,4096]{1,0:T(8,128)(2,1)} %get-tuple-element.55, bf16[4096,2048]{1,0:T(8,128)(2,1)} %shard_map.79.refs_1_, s32[]{:T(128)S(6)} %select_n.117), kind=kOutput, calls=%fused_computation.31 | convolution fusion | flops 34359738368 | bytes 58720260 | tf_op jit(solution)/shard_map/dot_general | solution.py:19
  567.8 106.9 %shard_map.80 = bf16[4096,4096]{1,0:T(8,128)(2,1)} custom-call(bf16[4096,2048]{1,0:T(8,128)(2,1)} %all-gather.14.cloned.1.call-done.refs_0_, bf16[4096,2048]{1,0:T(8,128)(2,1)} %shard_map.79.refs_1_, f32[4096,4096]{1,0:T(8,128)} %get-tuple-element.45.refs_2_), custom_call_target="tpu_custom_call" | custom-call | flops 68719476736 | bytes 100663296 | tf_op jit(solution)/shard_map/pallas_call | solution.py:137
  674.7 43.4 %fusion.37 = f32[4096,1024]{1,0:T(8,128)} fusion(bf16[4096,4096]{1,0:T(8,128)(2,1)} %shard_map.80, bf16[2048,4096]{1,0:T(8,128)(2,1)} %shard_map.75.refs_3_, s32[]{:T(128)S(6)} %select_n.117), kind=kOutput, calls=%fused_computation.39 | convolution fusion | flops 34359738368 | bytes 58720260 | tf_op jit(solution)/shard_map/dot_general | solution.py:19
  728.5 91.7 %collective-permute-done.9.refs_0_ = bf16[2048,1024]{1,0:T(8,128)(2,1)} collective-permute-done((bf16[2048,1024]{1,0:T(8,128)(2,1)}, bf16[2048,1024]{1,0:T(8,128)(2,1)}, u32[]{:S(2)}, u32[]{:S(2)}) %collective-permute-start.9) | collective-permute-done | bytes 4194336 | tf_op jit(solution)/shard_map/ppermute | solution.py:160
  820.2 84.5 %collective-permute-done.10.refs_1_ = bf16[2048,1024]{1,0:T(8,128)(2,1)} collective-permute-done((bf16[2048,1024]{1,0:T(8,128)(2,1)}, bf16[2048,1024]{1,0:T(8,128)(2,1)}, u32[]{:S(2)}, u32[]{:S(2)}) %collective-permute-start.10) | collective-permute-done | bytes 4194336 | tf_op jit(solution)/shard_map/ppermute | solution.py:160
  914.5 47.8 %fusion.40 = f32[4096,1024]{1,0:T(8,128)} fusion(bf16[4096,4096]{1,0:T(8,128)(2,1)} %shard_map.80, bf16[2048,4096]{1,0:T(8,128)(2,1)} %shard_map.75.refs_3_, s32[]{:T(128)S(6)} %select_n.113), kind=kOutput, calls=%fused_computation.42 | convolution fusion | flops 34359738368 | bytes 58720260 | tf_op jit(solution)/shard_map/dot_general | solution.py:19
  973.0 180.6 %shard_map.83 = (bf16[4096,4096]{1,0:T(8,128)(2,1)}, bf16[4096,4096]{1,0:T(8,128)(2,1)}) custom-call(bf16[4096,2048]{1,0:T(8,128)(2,1)} %all-gather.16.cloned.1.call-done.refs_0_, bf16[4096,2048]{1,0:T(8,128)(2,1)} %shard_map.79.refs_1_, bf16[4096,2048]{1,0:T(8,128)(2,1)} %all-gather.18.cloned.1.call-done.refs_2_, bf16[2048,4096]{1,0:T(8,128)(2,1)} %shard_map.75.refs_3_), custom_call_target="tpu_custom_call" | custom-call | flops 137438953472 | bytes 100663296 | tf_op jit(solution)/shard_map/pallas_call | solution.py:137
  1168.8 15.8 fusion.43
  1214.2 42.8 %convolution_add_fusion.1.refs_0_ = f32[4096,1024]{1,0:T(8,128)} fusion(f32[4096,1024]{1,0:T(8,128)} %fusion.70, bf16[4096,4096]{1,0:T(8,128)(2,1)} %get-tuple-element.56, bf16[4096,2048]{1,0:T(8,128)(2,1)} %all-gather.16.cloned.1.call-done.refs_0_, s32[]{:T(128)S(6)} %select_n.113), kind=kOutput, calls=%fused_computation.11 | convolution fusion | flops 34363932672 | bytes 75497472 | tf_op jit(solution)/shard_map/dot_general | solution.py:19
  1256.9 131.0 %collective-permute-done.6 = f32[2048,1024]{1,0:T(8,128)} collective-permute-done((f32[2048,1024]{1,0:T(8,128)}, f32[2048,1024]{1,0:T(8,128)}, u32[]{:S(2)}, u32[]{:S(2)}) %collective-permute-start.6) | collective-permute-done | bytes 8388640 | tf_op jit(solution)/shard_map/ppermute | solution.py:160
  1397.2 44.0 %fusion.14 = f32[1024,4096]{1,0:T(8,128)} fusion(bf16[4096,4096]{1,0:T(8,128)(2,1)} %shard_map.80, bf16[4096,2048]{1,0:T(8,128)(2,1)} %all-gather.20.cloned.1.call-done, s32[]{:T(128)S(6)} %select_n.122), kind=kOutput, calls=%fused_computation.19 | convolution fusion | flops 34359738368 | bytes 58720260 | tf_op jit(solution)/shard_map/dot_general | solution.py:19
  1441.2 43.1 %fusion.27 = f32[1024,4096]{1,0:T(8,128)} fusion(f32[1024,4096]{1,0:T(8,128)} %fusion.14, bf16[4096,4096]{1,0:T(8,128)(2,1)} %get-tuple-element.53, bf16[4096,2048]{1,0:T(8,128)(2,1)} %all-gather.18.cloned.1.call-done.refs_2_, s32[]{:T(128)S(6)} %select_n.122), kind=kOutput, calls=%fused_computation.33 | convolution fusion | flops 34363932672 | bytes 75497472 | tf_op jit(solution)/shard_map/dot_general | solution.py:19
  1493.5 219.3 %collective-permute-done.20.refs_5_ = f32[512,1024]{1,0:T(8,128)S(1)} collective-permute-done((f32[512,1024]{1,0:T(8,128)S(1)}, f32[512,1024]{1,0:T(8,128)S(1)}, u32[]{:S(2)}, u32[]{:S(2)}) %collective-permute-start.20) | collective-permute-done | bytes 2097184 | tf_op jit(solution)/shard_map/ppermute | solution.py:160
  1714.6 43.3 %collective-permute-done.18.refs_4_ = f32[512,1024]{1,0:T(8,128)} collective-permute-done((f32[512,1024]{1,0:T(8,128)S(1)}, f32[512,1024]{1,0:T(8,128)}, u32[]{:S(2)}, u32[]{:S(2)}) %collective-permute-start.18) | collective-permute-done | bytes 2097184 | tf_op jit(solution)/shard_map/ppermute | solution.py:160
  1757.9 44.9 %collective-permute-done.16.refs_3_ = f32[512,1024]{1,0:T(8,128)} collective-permute-done((f32[512,1024]{1,0:T(8,128)S(1)}, f32[512,1024]{1,0:T(8,128)}, u32[]{:S(2)}, u32[]{:S(2)}) %collective-permute-start.16) | collective-permute-done | bytes 2097184 | tf_op jit(solution)/shard_map/ppermute | solution.py:160
  1804.8 42.4 %collective-permute-done.14.refs_2_ = f32[512,1024]{1,0:T(8,128)S(1)} collective-permute-done((f32[512,1024]{1,0:T(8,128)S(1)}, f32[512,1024]{1,0:T(8,128)S(1)}, u32[]{:S(2)}, u32[]{:S(2)}) %collective-permute-start.14) | collective-permute-done | bytes 2097184 | tf_op jit(solution)/shard_map/ppermute | solution.py:160
  1877.6 20.9 collective-permute-done.19.refs_4_
  1900.2 43.6 %fusion.10 = f32[1024,4096]{1,0:T(8,128)} fusion(bf16[4096,4096]{1,0:T(8,128)(2,1)} %shard_map.80, bf16[4096,2048]{1,0:T(8,128)(2,1)} %all-gather.20.cloned.1.call-done, s32[]{:T(128)S(6)} %select_n.123), kind=kOutput, calls=%fused_computation.14 | convolution fusion | flops 34359738368 | bytes 58720260 | tf_op jit(solution)/shard_map/dot_general | solution.py:19
  1944.3 41.4 %collective-permute-done.15.refs_2_ = f32[512,1024]{1,0:T(8,128)} collective-permute-done((f32[512,1024]{1,0:T(8,128)S(1)}, f32[512,1024]{1,0:T(8,128)}, u32[]{:S(2)}, u32[]{:S(2)}) %collective-permute-start.15) | collective-permute-done | bytes 2097184 | tf_op jit(solution)/shard_map/ppermute | solution.py:160
  1986.2 43.1 %fusion.30.refs_0_ = f32[1024,4096]{1,0:T(8,128)} fusion(f32[1024,4096]{1,0:T(8,128)} %fusion.10, bf16[4096,4096]{1,0:T(8,128)(2,1)} %get-tuple-element.53, bf16[4096,2048]{1,0:T(8,128)(2,1)} %all-gather.18.cloned.1.call-done.refs_2_, s32[]{:T(128)S(6)} %select_n.123), kind=kOutput, calls=%fused_computation.34 | convolution fusion | flops 34363932672 | bytes 75497472 | tf_op jit(solution)/shard_map/dot_general | solution.py:19
  2029.4 24.3 %shard_map.85 = f32[1024,8192]{1,0:T(8,128)} custom-call(s32[6]{0:T(128)} %get-tuple-element.72.tab, f32[1024,4096]{1,0:T(8,128)} %fusion.30.refs_0_, f32[1024,4096]{1,0:T(8,128)} %collective-permute-done.12.refs_1_), custom_call_target="tpu_custom_call" | custom-call | flops 3355443200 | bytes 67108864 | tf_op jit(solution)/shard_map/pallas_call | solution.py:80
  2053.6 33.7 %shard_map.86.refs_10_ = f32[8192,1024]{1,0:T(8,128)} custom-call(s32[30]{0:T(128)} %stack.178.tab, f32[4096,1024]{1,0:T(8,128)} %convolution_add_fusion.1.refs_0_, f32[4096,1024]{1,0:T(8,128)} %collective-permute-done.13.refs_1_, f32[512,1024]{1,0:T(8,128)} %copy-done.2, f32[512,1024]{1,0:T(8,128)} %collective-permute-done.16.refs_3_, ...), custom_call_target="tpu_custom_call" | custom-call | flops 3355443200 | bytes 67108864 | tf_op jit(solution)/shard_map/pallas_call | solution.py:80
  2087.4 20.3 shard_map.87
  (137 shorter events, 209.5 us)
Async XLA Ops:
  16.0 139.5 %all-gather.10.cloned.1.call-start = ((), (), s32[]{:S(2)}) async-start(), calls=%async_computation.5 | async-start | bytes 12582912 | tf_op jit(solution)/shard_map/all_gather | solution.py:163
  16.0 94.1 %collective-permute-start.1 = (bf16[2048,1024]{1,0:T(8,128)(2,1)}, bf16[2048,1024]{1,0:T(8,128)(2,1)}, u32[]{:S(2)}, u32[]{:S(2)}) collective-permute-start(bf16[2048,1024]{1,0:T(8,128)(2,1)} %refs_0_.7), channel_id=1, source_target_pairs={{0,2},{2,0},{1,3},{3,1},{4,6},{6,4},{5,7},{7,5}} | collective-permute-start | bytes 12582920 | tf_op jit(solution)/shard_map/ppermute | solution.py:160
  110.1 160.8 %all-gather.12.cloned.1.call-start = ((), (), s32[]{:S(2)}) async-start(), calls=%async_computation.6 | async-start | bytes 12582912 | tf_op jit(solution)/shard_map/all_gather | solution.py:163
  118.9 448.9 %all-gather.14.cloned.1.call-start = ((), (), s32[]{:S(2)}) async-start(), calls=%async_computation.7 | async-start | bytes 25165824 | tf_op jit(solution)/shard_map/all_gather | solution.py:163
  144.3 170.3 %collective-permute-start.3 = (bf16[2048,1024]{1,0:T(8,128)(2,1)}, bf16[2048,1024]{1,0:T(8,128)(2,1)}, u32[]{:S(2)}, u32[]{:S(2)}) collective-permute-start(bf16[2048,1024]{1,0:T(8,128)(2,1)} %refs_0_.6), channel_id=1, source_target_pairs={{0,2},{2,0},{1,3},{3,1},{4,6},{6,4},{5,7},{7,5}} | collective-permute-start | bytes 12582920 | tf_op jit(solution)/shard_map/ppermute | solution.py:160
  322.9 650.1 %all-gather.16.cloned.1.call-start = ((), (), s32[]{:S(2)}) async-start(), calls=%async_computation.10 | async-start | bytes 25165824 | tf_op jit(solution)/shard_map/all_gather | solution.py:163
  322.9 92.3 %collective-permute-start.4 = (bf16[2048,1024]{1,0:T(8,128)(2,1)}, bf16[2048,1024]{1,0:T(8,128)(2,1)}, u32[]{:S(2)}, u32[]{:S(2)}) collective-permute-start(bf16[2048,1024]{1,0:T(8,128)(2,1)} %shard_map.77), channel_id=1, source_target_pairs={{0,2},{2,0},{1,3},{3,1},{4,6},{6,4},{5,7},{7,5}} | collective-permute-start | bytes 12582920 | tf_op jit(solution)/shard_map/ppermute | solution.py:160
  415.3 93.8 %collective-permute-start.5 = (bf16[2048,1024]{1,0:T(8,128)(2,1)}, bf16[2048,1024]{1,0:T(8,128)(2,1)}, u32[]{:S(2)}, u32[]{:S(2)}) collective-permute-start(bf16[2048,1024]{1,0:T(8,128)(2,1)} %collective-permute-done.4.refs_1_), channel_id=1, source_target_pairs={{0,4},{4,0},{1,5},{5,1},{2,6},{6,2},{3,7},{7,3}} | collective-permute-start | bytes 12582920 | tf_op jit(solution)/shard_map/ppermute | solution.py:160
  417.2 300.8 %collective-permute-start.7 = (bf16[2048,1024]{1,0:T(8,128)(2,1)}, bf16[2048,1024]{1,0:T(8,128)(2,1)}, u32[]{:S(2)}, u32[]{:S(2)}) collective-permute-start(bf16[2048,1024]{1,0:T(8,128)(2,1)} %refs_0_.6), channel_id=1, source_target_pairs={{0,4},{4,0},{1,5},{5,1},{2,6},{6,2},{3,7},{7,3}} | collective-permute-start | bytes 12582920 | tf_op jit(solution)/shard_map/ppermute | solution.py:160
  417.9 300.2 %collective-permute-start.8 = (bf16[2048,1024]{1,0:T(8,128)(2,1)}, bf16[2048,1024]{1,0:T(8,128)(2,1)}, u32[]{:S(2)}, u32[]{:S(2)}) collective-permute-start(bf16[2048,1024]{1,0:T(8,128)(2,1)} %collective-permute-done.3.refs_1_), channel_id=1, source_target_pairs={{0,4},{4,0},{1,5},{5,1},{2,6},{6,2},{3,7},{7,3}} | collective-permute-start | bytes 12582920 | tf_op jit(solution)/shard_map/ppermute | solution.py:160
  726.4 246.6 %all-gather.18.cloned.1.call-start = ((), (), s32[]{:S(2)}) async-start(), calls=%async_computation.11 | async-start | bytes 25165824 | tf_op jit(solution)/shard_map/all_gather | solution.py:163
  726.4 93.8 %collective-permute-start.9 = (bf16[2048,1024]{1,0:T(8,128)(2,1)}, bf16[2048,1024]{1,0:T(8,128)(2,1)}, u32[]{:S(2)}, u32[]{:S(2)}) collective-permute-start(bf16[2048,1024]{1,0:T(8,128)(2,1)} %refs_0_.7), channel_id=1, source_target_pairs={{0,4},{4,0},{1,5},{5,1},{2,6},{6,2},{3,7},{7,3}} | collective-permute-start | bytes 12582920 | tf_op jit(solution)/shard_map/ppermute | solution.py:160
  727.8 176.8 %collective-permute-start.10 = (bf16[2048,1024]{1,0:T(8,128)(2,1)}, bf16[2048,1024]{1,0:T(8,128)(2,1)}, u32[]{:S(2)}, u32[]{:S(2)}) collective-permute-start(bf16[2048,1024]{1,0:T(8,128)(2,1)} %collective-permute-done.1.refs_1_), channel_id=1, source_target_pairs={{0,4},{4,0},{1,5},{5,1},{2,6},{6,2},{3,7},{7,3}} | collective-permute-start | bytes 12582920 | tf_op jit(solution)/shard_map/ppermute | solution.py:160
  912.9 300.2 %reduce-scatter.7.cloned.1.call-start = ((), (), s32[]{:S(2)}) async-start(), calls=%async_computation.9 | async-start | bytes 25165824 | tf_op jit(solution)/shard_map/reduce_scatter | solution.py:166
  913.7 474.3 %reduce-scatter.5.cloned.1.call-start = ((), (), s32[]{:S(2)}) async-start(), calls=%async_computation.8 | async-start | bytes 25165824 | tf_op jit(solution)/shard_map/reduce_scatter | solution.py:166
  914.4 482.8 %all-gather.20.cloned.1.call-start = ((), (), s32[]{:S(2)}) async-start(), calls=%async_computation.14 | async-start | bytes 25165824 | tf_op jit(solution)/shard_map/all_gather | solution.py:163
  971.6 512.8 %reduce-scatter.11.cloned.1.call-start = ((), (), s32[]{:S(2)}) async-start(), calls=%async_computation.13 | async-start | bytes 25165824 | tf_op jit(solution)/shard_map/reduce_scatter | solution.py:166
  972.2 880.6 %reduce-scatter.9.cloned.1.call-start = ((), (), s32[]{:S(2)}) async-start(), calls=%async_computation.12 | async-start | bytes 25165824 | tf_op jit(solution)/shard_map/reduce_scatter | solution.py:166
  1213.1 174.8 %collective-permute-start.6 = (f32[2048,1024]{1,0:T(8,128)}, f32[2048,1024]{1,0:T(8,128)}, u32[]{:S(2)}, u32[]{:S(2)}) collective-permute-start(f32[2048,1024]{1,0:T(8,128)} %reduce-scatter.7.cloned.1.call-done), channel_id=1, source_target_pairs={{0,2},{2,0},{1,3},{3,1},{4,6},{6,4},{5,7},{7,5}} | collective-permute-start | bytes 25165832 | tf_op jit(solution)/shard_map/ppermute | solution.py:160
  1484.3 501.4 %collective-permute-start.12 = (f32[1024,4096]{1,0:T(8,128)}, f32[1024,4096]{1,0:T(8,128)}, u32[]{:S(2)}, u32[]{:S(2)}) collective-permute-start(f32[1024,4096]{1,0:T(8,128)} %fusion.27), channel_id=1, source_target_pairs={{0,1},{1,0},{2,3},{3,2},{4,5},{5,4},{6,7},{7,6}} | collective-permute-start | bytes 50331656 | tf_op jit(solution)/shard_map/ppermute | solution.py:160
  1484.4 367.0 %collective-permute-start.11 = (f32[2048,1024]{1,0:T(8,128)}, f32[2048,1024]{1,0:T(8,128)}, u32[]{:S(2)}, u32[]{:S(2)}) collective-permute-start(f32[2048,1024]{1,0:T(8,128)} %reduce-scatter.11.cloned.1.call-done), channel_id=1, source_target_pairs={{0,2},{2,0},{1,3},{3,1},{4,6},{6,4},{5,7},{7,5}} | collective-permute-start | bytes 25165832 | tf_op jit(solution)/shard_map/ppermute | solution.py:160
  1488.7 224.2 %collective-permute-start.20 = (f32[512,1024]{1,0:T(8,128)S(1)}, f32[512,1024]{1,0:T(8,128)S(1)}, u32[]{:S(2)}, u32[]{:S(2)}) collective-permute-start(f32[512,1024]{1,0:T(8,128)S(1)} %get-tuple-element.68), channel_id=1, source_target_pairs={{0,2},{2,0},{1,3},{3,1},{4,6},{6,4},{5,7},{7,5}} | collective-permute-start | bytes 6291464 | tf_op jit(solution)/shard_map/ppermute | solution.py:160
  1491.5 266.4 %collective-permute-start.18 = (f32[512,1024]{1,0:T(8,128)S(1)}, f32[512,1024]{1,0:T(8,128)}, u32[]{:S(2)}, u32[]{:S(2)}) collective-permute-start(f32[512,1024]{1,0:T(8,128)S(1)} %get-tuple-element.69), channel_id=1, source_target_pairs={{0,2},{2,0},{1,3},{3,1},{4,6},{6,4},{5,7},{7,5}} | collective-permute-start | bytes 6291464 | tf_op jit(solution)/shard_map/ppermute | solution.py:160
  1493.3 309.6 %collective-permute-start.16 = (f32[512,1024]{1,0:T(8,128)S(1)}, f32[512,1024]{1,0:T(8,128)}, u32[]{:S(2)}, u32[]{:S(2)}) collective-permute-start(f32[512,1024]{1,0:T(8,128)S(1)} %get-tuple-element.70), channel_id=1, source_target_pairs={{0,2},{2,0},{1,3},{3,1},{4,6},{6,4},{5,7},{7,5}} | collective-permute-start | bytes 6291464 | tf_op jit(solution)/shard_map/ppermute | solution.py:160
  1712.9 134.3 %collective-permute-start.14 = (f32[512,1024]{1,0:T(8,128)S(1)}, f32[512,1024]{1,0:T(8,128)S(1)}, u32[]{:S(2)}, u32[]{:S(2)}) collective-permute-start(f32[512,1024]{1,0:T(8,128)S(1)} %get-tuple-element.71), channel_id=1, source_target_pairs={{0,2},{2,0},{1,3},{3,1},{4,6},{6,4},{5,7},{7,5}} | collective-permute-start | bytes 6291464 | tf_op jit(solution)/shard_map/ppermute | solution.py:160
  1757.9 89.3 %collective-permute-start.29 = (f32[512,1024]{1,0:T(8,128)S(1)}, f32[512,1024]{1,0:T(8,128)S(1)}, u32[]{:S(2)}, u32[]{:S(2)}) collective-permute-start(f32[512,1024]{1,0:T(8,128)S(1)} %collective-permute-done.20.refs_5_), channel_id=1, source_target_pairs={{0,1},{1,0},{2,3},{3,2},{4,5},{5,4},{6,7},{7,6}} | collective-permute-start | bytes 6291464 | tf_op jit(solution)/shard_map/ppermute | solution.py:160
  1847.2 206.5 %collective-permute-start.13 = (f32[4096,1024]{1,0:T(8,128)}, f32[4096,1024]{1,0:T(8,128)}, u32[]{:S(2)}, u32[]{:S(2)}) collective-permute-start(f32[4096,1024]{1,0:T(8,128)} %convolution_add_fusion.1.refs_0_), channel_id=1, source_target_pairs={{0,1},{1,0},{2,3},{3,2},{4,5},{5,4},{6,7},{7,6}} | collective-permute-start | bytes 50331656 | tf_op jit(solution)/shard_map/ppermute | solution.py:160
  1898.4 87.3 %collective-permute-start.15 = (f32[512,1024]{1,0:T(8,128)S(1)}, f32[512,1024]{1,0:T(8,128)}, u32[]{:S(2)}, u32[]{:S(2)}) collective-permute-start(f32[512,1024]{1,0:T(8,128)S(1)} %copy-done.3), channel_id=1, source_target_pairs={{0,4},{4,0},{1,5},{5,1},{2,6},{6,2},{3,7},{7,3}} | collective-permute-start | bytes 6291464 | tf_op jit(solution)/shard_map/ppermute | solution.py:160
  1943.8 143.6 %collective-permute-start.25 = (f32[512,1024]{1,0:T(8,128)S(1)}, f32[512,1024]{1,0:T(8,128)}, u32[]{:S(2)}, u32[]{:S(2)}) collective-permute-start(f32[512,1024]{1,0:T(8,128)S(1)} %collective-permute-done.21.refs_5_), channel_id=1, source_target_pairs={{0,1},{1,0},{2,3},{3,2},{4,5},{5,4},{6,7},{7,6}} | collective-permute-start | bytes 6291464 | tf_op jit(solution)/shard_map/ppermute | solution.py:160
  1944.0 143.3 %collective-permute-start.24 = (f32[512,1024]{1,0:T(8,128)}, f32[512,1024]{1,0:T(8,128)}, u32[]{:S(2)}, u32[]{:S(2)}) collective-permute-start(f32[512,1024]{1,0:T(8,128)} %collective-permute-done.19.refs_4_), channel_id=1, source_target_pairs={{0,1},{1,0},{2,3},{3,2},{4,5},{5,4},{6,7},{7,6}} | collective-permute-start | bytes 6291464 | tf_op jit(solution)/shard_map/ppermute | solution.py:160
  1985.7 101.7 %collective-permute-start.23 = (f32[512,1024]{1,0:T(8,128)}, f32[512,1024]{1,0:T(8,128)}, u32[]{:S(2)}, u32[]{:S(2)}) collective-permute-start(f32[512,1024]{1,0:T(8,128)} %collective-permute-done.17.refs_3_), channel_id=1, source_target_pairs={{0,1},{1,0},{2,3},{3,2},{4,5},{5,4},{6,7},{7,6}} | collective-permute-start | bytes 6291464 | tf_op jit(solution)/shard_map/ppermute | solution.py:160
  1985.7 101.7 %collective-permute-start.22 = (f32[512,1024]{1,0:T(8,128)}, f32[512,1024]{1,0:T(8,128)}, u32[]{:S(2)}, u32[]{:S(2)}) collective-permute-start(f32[512,1024]{1,0:T(8,128)} %collective-permute-done.15.refs_2_), channel_id=1, source_target_pairs={{0,1},{1,0},{2,3},{3,2},{4,5},{5,4},{6,7},{7,6}} | collective-permute-start | bytes 6291464 | tf_op jit(solution)/shard_map/ppermute | solution.py:160
  (24 other events, 1509.2 us)
Sparse Core Ops, SparseCore 0:
  16.1 19.1 all-gather.7
  110.2 23.5 all-gather.9
  135.3 18.2 all-gather.11
  323.0 27.0 all-gather.13
  726.5 27.3 all-gather.15
  913.0 28.4 all-gather.17
  943.8 23.3 reduce-scatter.6
  969.5 23.5 reduce-scatter.4
  994.6 28.6 all-gather.19
  1025.4 23.3 reduce-scatter.10
  1051.1 23.5 reduce-scatter.8

commit v4 on v3

--- a/solution.py
+++ b/solution.py
@@ -175,9 +175,10 @@
         w2_core = swap(w2_cut, "row")
         w1_core = swap(w1_cut, "row")
         step = 1024
-        w2_fwd = lay([(w_out, jnp.where(stay, -1, 0), half, r * ffn + d * half, (0, hid)), (w2_core, jnp.where(stay, 0, -1), half, d * half, (0, hid))], half, hid, step)
         per1 = hid // 256
         w1 = lay([(w_in, r * per1, hid, 0, (r, ffn)), whole(w1_core, (1 - r) * per1)], 2 * hid, ffn, 256)
+        w2_core = after(w2_core, w1)
+        w2_fwd = lay([(w_out, jnp.where(stay, -1, 0), half, r * ffn + d * half, (0, hid)), (w2_core, jnp.where(stay, 0, -1), half, d * half, (0, hid))], half, hid, step)
         w2_a = swap(w2_fwd, "col")
         grad_x = swap(after(grad, w2_fwd), "col")
         tok_xy = swap(tok_x, "depth")
@@ -197,8 +198,9 @@
         w2 = lay([whole(w2_own, c * per2), whole(w2_a, (1 - c) * per2 + d * (per2 // 2)), whole(after(w2_b, dw2_near), (1 - c) * per2 + (1 - d) * (per2 // 2))], ffn, 2 * hid, step)
         y_oth = dot(a_near, part(w2, 1 - c, hid, 1), 1, 0)
         y_got = swap(over_cores(y_oth), "col")
-        x_far = cores(join_cols(after(tok_y, y_oth), tok_xy, c, step))
-        (du_near,) = ffn_kernel(after(g_near, y_oth), w2, pre=pre)
+        tok_far = join_cols(after(tok_y, y_oth), tok_xy, c, step)
+        x_far = cores(tok_far)
+        (du_near,) = ffn_kernel(after(g_near, y_oth, tok_far), w2, pre=pre)
         y_mine = over_cores(after(y_own, du_near))
         dx_oth = dot(du_near, part(w1, 1 - c, hid, 0), 1, 1)
         dx_got = swap(over_cores(dx_oth), "col")

time: 2120 us -> 2090 us (0.986)
  waiting for transfers between devices: 968 us -> 936 us
    ppermute x30, waiting for transfers between devices: 966 us -> 933 us  [swap(): return lax.ppermute(v, axis, SWAP)]
  transfers between devices with their start and end apart: 41 -> 41, of which waited for: 16 -> 17; matrix products, arithmetic and copies ran while one was open for 31% -> 31% of each run, Pallas kernels for 19% -> 20%
where the time goes in v4:
time: 2090 us; the launch traced here: 2080 us
  waiting for transfers between devices  936 us (45%)
  matrix products  614 us (29%)
  Pallas kernels  446 us (21%)
  starting transfers between devices  26.4 us (1%)
  local copies, waits for them, and re-layouts  26.2 us (1%)
    ppermute x30, waiting for transfers between devices, swap(): return lax.ppermute(v, axis, SWAP)  933 us
    dot_general x16, matrix products, dot(): lax.dot_general(lhs, rhs, (((lc,), (rc,)), ((), ())), preferred_element_t...  614 us
    pallas_call x2, Pallas kernels, ffn_kernel(): pl.pallas_call(body, grid=(ffn // tn, rows // tm), in_specs=in_specs, out...  288 us
    pallas_call x11, Pallas kernels, lay(): pl.pallas_call(body, out_shape=jax.ShapeDtypeStruct((out_rows, out_cols),...  158 us
  transfers between devices with their start and end apart: 41, of which 17 were waited for; matrix products, arithmetic and copies ran while one was open for 31% of the time, Pallas kernels for 20%

profile of v4, /device:TPU:0, one launch (start us, length us, event | category | flops | bytes accessed | tf_op | source)
XLA Modules:
  0.0 2082.3 jit_solution(16522591717258055941)
XLA Ops:
  44.8 43.9 %convolution_bitcast_fusion = f32[4096,4096]{1,0:T(8,128)} fusion(bf16[4096,1024]{1,0:T(8,128)(2,1)} %all-gather.8.cloned.1.call-done, bf16[2048,4096]{1,0:T(8,128)(2,1)} %shard_map.75.refs_3_, s32[]{:T(128)S(6)} %select_n.113), kind=kOutput, calls=%fused_computation.10 | convolution fusion | flops 34359738368 | bytes 83886080 | tf_op jit(solution)/shard_map/dot_general | solution.py:19
  88.8 21.3 %collective-permute-done.1.refs_1_ = bf16[2048,1024]{1,0:T(8,128)(2,1)} collective-permute-done((bf16[2048,1024]{1,0:T(8,128)(2,1)}, bf16[2048,1024]{1,0:T(8,128)(2,1)}, u32[]{:S(2)}, u32[]{:S(2)}) %collective-permute-start.1) | collective-permute-done | bytes 4194336 | tf_op jit(solution)/shard_map/ppermute | solution.py:160
  121.8 16.6 collective-permute-done.2.refs_1_
  155.5 72.0 %fusion.7 = (bf16[4096,4096]{1,0:T(8,128)(2,1)}, f32[4096,4096]{1,0:T(8,128)}) fusion(f32[4096,4096]{1,0:T(8,128)} %convolution_bitcast_fusion, bf16[4096,1024]{1,0:T(8,128)(2,1)} %all-gather.10.cloned.1.call-done, bf16[2048,4096]{1,0:T(8,128)(2,1)} %shard_map.75.refs_3_, s32[]{:T(128)S(6)} %select_n.117), kind=kOutput, calls=%fused_computation.8 | convolution fusion | flops 34527510528 | bytes 184549376 | tf_op jit(solution)/shard_map/dot_general | solution.py:19
  227.5 43.5 %fusion.69 = f32[4096,1024]{1,0:T(8,128)} fusion(bf16[4096,4096]{1,0:T(8,128)(2,1)} %get-tuple-element.57, bf16[4096,1024]{1,0:T(8,128)(2,1)} %shard_map.76.refs_0_), kind=kOutput, calls=%fused_computation.67 | convolution fusion | flops 34359738368 | bytes 58720256 | tf_op jit(solution)/shard_map/dot_general | solution.py:19
  271.0 43.7 %fusion.70 = f32[4096,1024]{1,0:T(8,128)} fusion(bf16[4096,4096]{1,0:T(8,128)(2,1)} %get-tuple-element.57, bf16[4096,1024]{1,0:T(8,128)(2,1)} %all-gather.12.cloned.1.call-done), kind=kOutput, calls=%fused_computation.68 | convolution fusion | flops 34359738368 | bytes 58720256 | tf_op jit(solution)/shard_map/dot_general | solution.py:19
  323.1 92.3 %collective-permute-done.4.refs_1_ = bf16[2048,1024]{1,0:T(8,128)(2,1)} collective-permute-done((bf16[2048,1024]{1,0:T(8,128)(2,1)}, bf16[2048,1024]{1,0:T(8,128)(2,1)}, u32[]{:S(2)}, u32[]{:S(2)}) %collective-permute-start.4) | collective-permute-done | bytes 4194336 | tf_op jit(solution)/shard_map/ppermute | solution.py:160
  421.5 87.6 %collective-permute-done.5.refs_2_ = bf16[2048,1024]{1,0:T(8,128)(2,1)} collective-permute-done((bf16[2048,1024]{1,0:T(8,128)(2,1)}, bf16[2048,1024]{1,0:T(8,128)(2,1)}, u32[]{:S(2)}, u32[]{:S(2)}) %collective-permute-start.5) | collective-permute-done | bytes 4194336 | tf_op jit(solution)/shard_map/ppermute | solution.py:160
  525.0 43.1 %fusion.25 = f32[4096,1024]{1,0:T(8,128)} fusion(bf16[4096,4096]{1,0:T(8,128)(2,1)} %get-tuple-element.57, bf16[4096,2048]{1,0:T(8,128)(2,1)} %shard_map.79.refs_1_, s32[]{:T(128)S(6)} %select_n.117), kind=kOutput, calls=%fused_computation.31 | convolution fusion | flops 34359738368 | bytes 58720260 | tf_op jit(solution)/shard_map/dot_general | solution.py:19
  568.1 30.9 %collective-permute-done.6.refs_0_ = bf16[2048,1024]{1,0:T(8,128)(2,1)} collective-permute-done((bf16[2048,1024]{1,0:T(8,128)(2,1)}, bf16[2048,1024]{1,0:T(8,128)(2,1)}, u32[]{:S(2)}, u32[]{:S(2)}) %collective-permute-start.6) | collective-permute-done | bytes 4194336 | tf_op jit(solution)/shard_map/ppermute | solution.py:160
  599.0 89.9 %collective-permute-done.7.refs_1_ = bf16[2048,1024]{1,0:T(8,128)(2,1)} collective-permute-done((bf16[2048,1024]{1,0:T(8,128)(2,1)}, bf16[2048,1024]{1,0:T(8,128)(2,1)}, u32[]{:S(2)}, u32[]{:S(2)}) %collective-permute-start.7) | collective-permute-done | bytes 4194336 | tf_op jit(solution)/shard_map/ppermute | solution.py:160
  697.2 106.9 %shard_map.81 = bf16[4096,4096]{1,0:T(8,128)(2,1)} custom-call(bf16[4096,2048]{1,0:T(8,128)(2,1)} %all-gather.14.cloned.1.call-done.refs_0_, bf16[4096,2048]{1,0:T(8,128)(2,1)} %shard_map.79.refs_1_, f32[4096,4096]{1,0:T(8,128)} %get-tuple-element.48.refs_2_), custom_call_target="tpu_custom_call" | custom-call | flops 68719476736 | bytes 100663296 | tf_op jit(solution)/shard_map/pallas_call | solution.py:137
  804.1 43.5 %fusion.37 = f32[4096,1024]{1,0:T(8,128)} fusion(bf16[4096,4096]{1,0:T(8,128)(2,1)} %shard_map.81, bf16[2048,4096]{1,0:T(8,128)(2,1)} %shard_map.75.refs_3_, s32[]{:T(128)S(6)} %select_n.117), kind=kOutput, calls=%fused_computation.39 | convolution fusion | flops 34359738368 | bytes 58720260 | tf_op jit(solution)/shard_map/dot_general | solution.py:19
  847.6 18.8 collective-permute-done.10.refs_1_
  876.8 47.9 %fusion.40 = f32[4096,1024]{1,0:T(8,128)} fusion(bf16[4096,4096]{1,0:T(8,128)(2,1)} %shard_map.81, bf16[2048,4096]{1,0:T(8,128)(2,1)} %shard_map.75.refs_3_, s32[]{:T(128)S(6)} %select_n.113), kind=kOutput, calls=%fused_computation.42 | convolution fusion | flops 34359738368 | bytes 58720260 | tf_op jit(solution)/shard_map/dot_general | solution.py:19
  934.3 181.2 %shard_map.83 = (bf16[4096,4096]{1,0:T(8,128)(2,1)}, bf16[4096,4096]{1,0:T(8,128)(2,1)}) custom-call(bf16[4096,2048]{1,0:T(8,128)(2,1)} %all-gather.16.cloned.1.call-done.refs_0_, bf16[4096,2048]{1,0:T(8,128)(2,1)} %shard_map.79.refs_1_, bf16[4096,2048]{1,0:T(8,128)(2,1)} %all-gather.18.cloned.1.call-done.refs_2_, bf16[2048,4096]{1,0:T(8,128)(2,1)} %shard_map.75.refs_3_), custom_call_target="tpu_custom_call" | custom-call | flops 137438953472 | bytes 100663296 | tf_op jit(solution)/shard_map/pallas_call | solution.py:137
  1130.8 15.8 fusion.43
  1175.8 42.8 %convolution_add_fusion.1.refs_0_ = f32[4096,1024]{1,0:T(8,128)} fusion(f32[4096,1024]{1,0:T(8,128)} %fusion.70, bf16[4096,4096]{1,0:T(8,128)(2,1)} %get-tuple-element.58, bf16[4096,2048]{1,0:T(8,128)(2,1)} %all-gather.16.cloned.1.call-done.refs_0_, s32[]{:T(128)S(6)} %select_n.113), kind=kOutput, calls=%fused_computation.11 | convolution fusion | flops 34363932672 | bytes 75497472 | tf_op jit(solution)/shard_map/dot_general | solution.py:19
  1218.5 137.3 %collective-permute-done.8 = f32[2048,1024]{1,0:T(8,128)} collective-permute-done((f32[2048,1024]{1,0:T(8,128)}, f32[2048,1024]{1,0:T(8,128)}, u32[]{:S(2)}, u32[]{:S(2)}) %collective-permute-start.8) | collective-permute-done | bytes 8388640 | tf_op jit(solution)/shard_map/ppermute | solution.py:160
  1365.1 44.0 %fusion.14 = f32[1024,4096]{1,0:T(8,128)} fusion(bf16[4096,4096]{1,0:T(8,128)(2,1)} %shard_map.81, bf16[4096,2048]{1,0:T(8,128)(2,1)} %all-gather.20.cloned.1.call-done, s32[]{:T(128)S(6)} %select_n.122), kind=kOutput, calls=%fused_computation.19 | convolution fusion | flops 34359738368 | bytes 58720260 | tf_op jit(solution)/shard_map/dot_general | solution.py:19
  1409.1 43.1 %fusion.27 = f32[1024,4096]{1,0:T(8,128)} fusion(f32[1024,4096]{1,0:T(8,128)} %fusion.14, bf16[4096,4096]{1,0:T(8,128)(2,1)} %get-tuple-element.55, bf16[4096,2048]{1,0:T(8,128)(2,1)} %all-gather.18.cloned.1.call-done.refs_2_, s32[]{:T(128)S(6)} %select_n.122), kind=kOutput, calls=%fused_computation.33 | convolution fusion | flops 34363932672 | bytes 75497472 | tf_op jit(solution)/shard_map/dot_general | solution.py:19
  1461.5 219.3 %collective-permute-done.20.refs_5_ = f32[512,1024]{1,0:T(8,128)S(1)} collective-permute-done((f32[512,1024]{1,0:T(8,128)S(1)}, f32[512,1024]{1,0:T(8,128)S(1)}, u32[]{:S(2)}, u32[]{:S(2)}) %collective-permute-start.20) | collective-permute-done | bytes 2097184 | tf_op jit(solution)/shard_map/ppermute | solution.py:160
  1682.6 43.3 %collective-permute-done.18.refs_4_ = f32[512,1024]{1,0:T(8,128)} collective-permute-done((f32[512,1024]{1,0:T(8,128)S(1)}, f32[512,1024]{1,0:T(8,128)}, u32[]{:S(2)}, u32[]{:S(2)}) %collective-permute-start.18) | collective-permute-done | bytes 2097184 | tf_op jit(solution)/shard_map/ppermute | solution.py:160
  1725.9 44.9 %collective-permute-done.16.refs_3_ = f32[512,1024]{1,0:T(8,128)} collective-permute-done((f32[512,1024]{1,0:T(8,128)S(1)}, f32[512,1024]{1,0:T(8,128)}, u32[]{:S(2)}, u32[]{:S(2)}) %collective-permute-start.16) | collective-permute-done | bytes 2097184 | tf_op jit(solution)/shard_map/ppermute | solution.py:160
  1772.6 42.6 %collective-permute-done.14.refs_2_ = f32[512,1024]{1,0:T(8,128)S(1)} collective-permute-done((f32[512,1024]{1,0:T(8,128)S(1)}, f32[512,1024]{1,0:T(8,128)S(1)}, u32[]{:S(2)}, u32[]{:S(2)}) %collective-permute-start.14) | collective-permute-done | bytes 2097184 | tf_op jit(solution)/shard_map/ppermute | solution.py:160
  1845.4 20.9 %collective-permute-done.19.refs_4_ = f32[512,1024]{1,0:T(8,128)} collective-permute-done((f32[512,1024]{1,0:T(8,128)}, f32[512,1024]{1,0:T(8,128)}, u32[]{:S(2)}, u32[]{:S(2)}) %collective-permute-start.19) | collective-permute-done | bytes 2097184 | tf_op jit(solution)/shard_map/ppermute | solution.py:160
  1868.0 43.6 %fusion.10 = f32[1024,4096]{1,0:T(8,128)} fusion(bf16[4096,4096]{1,0:T(8,128)(2,1)} %shard_map.81, bf16[4096,2048]{1,0:T(8,128)(2,1)} %all-gather.20.cloned.1.call-done, s32[]{:T(128)S(6)} %select_n.123), kind=kOutput, calls=%fused_computation.14 | convolution fusion | flops 34359738368 | bytes 58720260 | tf_op jit(solution)/shard_map/dot_general | solution.py:19
  1912.1 41.3 %collective-permute-done.15.refs_2_ = f32[512,1024]{1,0:T(8,128)} collective-permute-done((f32[512,1024]{1,0:T(8,128)S(1)}, f32[512,1024]{1,0:T(8,128)}, u32[]{:S(2)}, u32[]{:S(2)}) %collective-permute-start.15) | collective-permute-done | bytes 2097184 | tf_op jit(solution)/shard_map/ppermute | solution.py:160
  1954.0 43.1 %fusion.30.refs_0_ = f32[1024,4096]{1,0:T(8,128)} fusion(f32[1024,4096]{1,0:T(8,128)} %fusion.10, bf16[4096,4096]{1,0:T(8,128)(2,1)} %get-tuple-element.55, bf16[4096,2048]{1,0:T(8,128)(2,1)} %all-gather.18.cloned.1.call-done.refs_2_, s32[]{:T(128)S(6)} %select_n.123), kind=kOutput, calls=%fused_computation.34 | convolution fusion | flops 34363932672 | bytes 75497472 | tf_op jit(solution)/shard_map/dot_general | solution.py:19
  1997.1 24.3 %shard_map.85 = f32[1024,8192]{1,0:T(8,128)} custom-call(s32[6]{0:T(128)} %get-tuple-element.74.tab, f32[1024,4096]{1,0:T(8,128)} %fusion.30.refs_0_, f32[1024,4096]{1,0:T(8,128)} %collective-permute-done.12.refs_1_), custom_call_target="tpu_custom_call" | custom-call | flops 3355443200 | bytes 67108864 | tf_op jit(solution)/shard_map/pallas_call | solution.py:80
  2021.4 33.7 %shard_map.86.refs_10_ = f32[8192,1024]{1,0:T(8,128)} custom-call(s32[30]{0:T(128)} %stack.178.tab, f32[4096,1024]{1,0:T(8,128)} %convolution_add_fusion.1.refs_0_, f32[4096,1024]{1,0:T(8,128)} %collective-permute-done.13.refs_1_, f32[512,1024]{1,0:T(8,128)} %copy-done.2, f32[512,1024]{1,0:T(8,128)} %collective-permute-done.16.refs_3_, ...), custom_call_target="tpu_custom_call" | custom-call | flops 3355443200 | bytes 67108864 | tf_op jit(solution)/shard_map/pallas_call | solution.py:80
  2055.1 20.4 shard_map.87
  (137 shorter events, 224.2 us)
Async XLA Ops:
  16.0 139.5 %all-gather.10.cloned.1.call-start = ((), (), s32[]{:S(2)}) async-start(), calls=%async_computation.5 | async-start | bytes 12582912 | tf_op jit(solution)/shard_map/all_gather | solution.py:163
  16.0 94.1 %collective-permute-start.1 = (bf16[2048,1024]{1,0:T(8,128)(2,1)}, bf16[2048,1024]{1,0:T(8,128)(2,1)}, u32[]{:S(2)}, u32[]{:S(2)}) collective-permute-start(bf16[2048,1024]{1,0:T(8,128)(2,1)} %refs_0_.7), channel_id=1, source_target_pairs={{0,2},{2,0},{1,3},{3,1},{4,6},{6,4},{5,7},{7,5}} | collective-permute-start | bytes 12582920 | tf_op jit(solution)/shard_map/ppermute | solution.py:160
  110.1 160.9 %all-gather.12.cloned.1.call-start = ((), (), s32[]{:S(2)}) async-start(), calls=%async_computation.6 | async-start | bytes 12582912 | tf_op jit(solution)/shard_map/all_gather | solution.py:163
  118.9 578.3 %all-gather.14.cloned.1.call-start = ((), (), s32[]{:S(2)}) async-start(), calls=%async_computation.7 | async-start | bytes 25165824 | tf_op jit(solution)/shard_map/all_gather | solution.py:163
  144.3 170.4 %collective-permute-start.3 = (bf16[2048,1024]{1,0:T(8,128)(2,1)}, bf16[2048,1024]{1,0:T(8,128)(2,1)}, u32[]{:S(2)}, u32[]{:S(2)}) collective-permute-start(bf16[2048,1024]{1,0:T(8,128)(2,1)} %refs_0_.6), channel_id=1, source_target_pairs={{0,2},{2,0},{1,3},{3,1},{4,6},{6,4},{5,7},{7,5}} | collective-permute-start | bytes 12582920 | tf_op jit(solution)/shard_map/ppermute | solution.py:160
  323.0 611.3 %all-gather.16.cloned.1.call-start = ((), (), s32[]{:S(2)}) async-start(), calls=%async_computation.10 | async-start | bytes 25165824 | tf_op jit(solution)/shard_map/all_gather | solution.py:163
  323.1 92.3 %collective-permute-start.4 = (bf16[2048,1024]{1,0:T(8,128)(2,1)}, bf16[2048,1024]{1,0:T(8,128)(2,1)}, u32[]{:S(2)}, u32[]{:S(2)}) collective-permute-start(bf16[2048,1024]{1,0:T(8,128)(2,1)} %shard_map.77), channel_id=1, source_target_pairs={{0,2},{2,0},{1,3},{3,1},{4,6},{6,4},{5,7},{7,5}} | collective-permute-start | bytes 12582920 | tf_op jit(solution)/shard_map/ppermute | solution.py:160
  415.4 93.8 %collective-permute-start.5 = (bf16[2048,1024]{1,0:T(8,128)(2,1)}, bf16[2048,1024]{1,0:T(8,128)(2,1)}, u32[]{:S(2)}, u32[]{:S(2)}) collective-permute-start(bf16[2048,1024]{1,0:T(8,128)(2,1)} %collective-permute-done.4.refs_1_), channel_id=1, source_target_pairs={{0,4},{4,0},{1,5},{5,1},{2,6},{6,2},{3,7},{7,3}} | collective-permute-start | bytes 12582920 | tf_op jit(solution)/shard_map/ppermute | solution.py:160
  416.8 182.2 %collective-permute-start.6 = (bf16[2048,1024]{1,0:T(8,128)(2,1)}, bf16[2048,1024]{1,0:T(8,128)(2,1)}, u32[]{:S(2)}, u32[]{:S(2)}) collective-permute-start(bf16[2048,1024]{1,0:T(8,128)(2,1)} %refs_0_.7), channel_id=1, source_target_pairs={{0,4},{4,0},{1,5},{5,1},{2,6},{6,2},{3,7},{7,3}} | collective-permute-start | bytes 12582920 | tf_op jit(solution)/shard_map/ppermute | solution.py:160
  418.1 270.8 %collective-permute-start.7 = (bf16[2048,1024]{1,0:T(8,128)(2,1)}, bf16[2048,1024]{1,0:T(8,128)(2,1)}, u32[]{:S(2)}, u32[]{:S(2)}) collective-permute-start(bf16[2048,1024]{1,0:T(8,128)(2,1)} %collective-permute-done.1.refs_1_), channel_id=1, source_target_pairs={{0,4},{4,0},{1,5},{5,1},{2,6},{6,2},{3,7},{7,3}} | collective-permute-start | bytes 12582920 | tf_op jit(solution)/shard_map/ppermute | solution.py:160
  419.5 428.1 %collective-permute-start.9 = (bf16[2048,1024]{1,0:T(8,128)(2,1)}, bf16[2048,1024]{1,0:T(8,128)(2,1)}, u32[]{:S(2)}, u32[]{:S(2)}) collective-permute-start(bf16[2048,1024]{1,0:T(8,128)(2,1)} %refs_0_.6), channel_id=1, source_target_pairs={{0,4},{4,0},{1,5},{5,1},{2,6},{6,2},{3,7},{7,3}} | collective-permute-start | bytes 12582920 | tf_op jit(solution)/shard_map/ppermute | solution.py:160
  420.1 446.2 %collective-permute-start.10 = (bf16[2048,1024]{1,0:T(8,128)(2,1)}, bf16[2048,1024]{1,0:T(8,128)(2,1)}, u32[]{:S(2)}, u32[]{:S(2)}) collective-permute-start(bf16[2048,1024]{1,0:T(8,128)(2,1)} %collective-permute-done.3.refs_1_), channel_id=1, source_target_pairs={{0,4},{4,0},{1,5},{5,1},{2,6},{6,2},{3,7},{7,3}} | collective-permute-start | bytes 12582920 | tf_op jit(solution)/shard_map/ppermute | solution.py:160
  875.2 299.9 %reduce-scatter.7.cloned.1.call-start = ((), (), s32[]{:S(2)}) async-start(), calls=%async_computation.9 | async-start | bytes 25165824 | tf_op jit(solution)/shard_map/reduce_scatter | solution.py:166
  876.0 479.9 %reduce-scatter.5.cloned.1.call-start = ((), (), s32[]{:S(2)}) async-start(), calls=%async_computation.8 | async-start | bytes 25165824 | tf_op jit(solution)/shard_map/reduce_scatter | solution.py:166
  876.7 488.4 %all-gather.20.cloned.1.call-start = ((), (), s32[]{:S(2)}) async-start(), calls=%async_computation.14 | async-start | bytes 25165824 | tf_op jit(solution)/shard_map/all_gather | solution.py:163
  933.0 519.4 %reduce-scatter.11.cloned.1.call-start = ((), (), s32[]{:S(2)}) async-start(), calls=%async_computation.13 | async-start | bytes 25165824 | tf_op jit(solution)/shard_map/reduce_scatter | solution.py:166
  933.6 887.1 %reduce-scatter.9.cloned.1.call-start = ((), (), s32[]{:S(2)}) async-start(), calls=%async_computation.12 | async-start | bytes 25165824 | tf_op jit(solution)/shard_map/reduce_scatter | solution.py:166
  1175.1 180.7 %collective-permute-start.8 = (f32[2048,1024]{1,0:T(8,128)}, f32[2048,1024]{1,0:T(8,128)}, u32[]{:S(2)}, u32[]{:S(2)}) collective-permute-start(f32[2048,1024]{1,0:T(8,128)} %reduce-scatter.7.cloned.1.call-done), channel_id=1, source_target_pairs={{0,2},{2,0},{1,3},{3,1},{4,6},{6,4},{5,7},{7,5}} | collective-permute-start | bytes 25165832 | tf_op jit(solution)/shard_map/ppermute | solution.py:160
  1452.3 501.2 %collective-permute-start.12 = (f32[1024,4096]{1,0:T(8,128)}, f32[1024,4096]{1,0:T(8,128)}, u32[]{:S(2)}, u32[]{:S(2)}) collective-permute-start(f32[1024,4096]{1,0:T(8,128)} %fusion.27), channel_id=1, source_target_pairs={{0,1},{1,0},{2,3},{3,2},{4,5},{5,4},{6,7},{7,6}} | collective-permute-start | bytes 50331656 | tf_op jit(solution)/shard_map/ppermute | solution.py:160
  1452.3 366.8 %collective-permute-start.11 = (f32[2048,1024]{1,0:T(8,128)}, f32[2048,1024]{1,0:T(8,128)}, u32[]{:S(2)}, u32[]{:S(2)}) collective-permute-start(f32[2048,1024]{1,0:T(8,128)} %reduce-scatter.11.cloned.1.call-done), channel_id=1, source_target_pairs={{0,2},{2,0},{1,3},{3,1},{4,6},{6,4},{5,7},{7,5}} | collective-permute-start | bytes 25165832 | tf_op jit(solution)/shard_map/ppermute | solution.py:160
  1456.6 224.2 %collective-permute-start.20 = (f32[512,1024]{1,0:T(8,128)S(1)}, f32[512,1024]{1,0:T(8,128)S(1)}, u32[]{:S(2)}, u32[]{:S(2)}) collective-permute-start(f32[512,1024]{1,0:T(8,128)S(1)} %get-tuple-element.70), channel_id=1, source_target_pairs={{0,2},{2,0},{1,3},{3,1},{4,6},{6,4},{5,7},{7,5}} | collective-permute-start | bytes 6291464 | tf_op jit(solution)/shard_map/ppermute | solution.py:160
  1459.5 266.4 %collective-permute-start.18 = (f32[512,1024]{1,0:T(8,128)S(1)}, f32[512,1024]{1,0:T(8,128)}, u32[]{:S(2)}, u32[]{:S(2)}) collective-permute-start(f32[512,1024]{1,0:T(8,128)S(1)} %get-tuple-element.71), channel_id=1, source_target_pairs={{0,2},{2,0},{1,3},{3,1},{4,6},{6,4},{5,7},{7,5}} | collective-permute-start | bytes 6291464 | tf_op jit(solution)/shard_map/ppermute | solution.py:160
  1461.2 309.6 %collective-permute-start.16 = (f32[512,1024]{1,0:T(8,128)S(1)}, f32[512,1024]{1,0:T(8,128)}, u32[]{:S(2)}, u32[]{:S(2)}) collective-permute-start(f32[512,1024]{1,0:T(8,128)S(1)} %get-tuple-element.72), channel_id=1, source_target_pairs={{0,2},{2,0},{1,3},{3,1},{4,6},{6,4},{5,7},{7,5}} | collective-permute-start | bytes 6291464 | tf_op jit(solution)/shard_map/ppermute | solution.py:160
  1680.8 134.3 %collective-permute-start.14 = (f32[512,1024]{1,0:T(8,128)S(1)}, f32[512,1024]{1,0:T(8,128)S(1)}, u32[]{:S(2)}, u32[]{:S(2)}) collective-permute-start(f32[512,1024]{1,0:T(8,128)S(1)} %get-tuple-element.73), channel_id=1, source_target_pairs={{0,2},{2,0},{1,3},{3,1},{4,6},{6,4},{5,7},{7,5}} | collective-permute-start | bytes 6291464 | tf_op jit(solution)/shard_map/ppermute | solution.py:160
  1725.9 89.3 %collective-permute-start.29 = (f32[512,1024]{1,0:T(8,128)S(1)}, f32[512,1024]{1,0:T(8,128)S(1)}, u32[]{:S(2)}, u32[]{:S(2)}) collective-permute-start(f32[512,1024]{1,0:T(8,128)S(1)} %collective-permute-done.20.refs_5_), channel_id=1, source_target_pairs={{0,1},{1,0},{2,3},{3,2},{4,5},{5,4},{6,7},{7,6}} | collective-permute-start | bytes 6291464 | tf_op jit(solution)/shard_map/ppermute | solution.py:160
  1815.1 206.2 %collective-permute-start.13 = (f32[4096,1024]{1,0:T(8,128)}, f32[4096,1024]{1,0:T(8,128)}, u32[]{:S(2)}, u32[]{:S(2)}) collective-permute-start(f32[4096,1024]{1,0:T(8,128)} %convolution_add_fusion.1.refs_0_), channel_id=1, source_target_pairs={{0,1},{1,0},{2,3},{3,2},{4,5},{5,4},{6,7},{7,6}} | collective-permute-start | bytes 50331656 | tf_op jit(solution)/shard_map/ppermute | solution.py:160
  1843.6 68.0 %collective-permute-start.17 = (f32[512,1024]{1,0:T(8,128)}, f32[512,1024]{1,0:T(8,128)}, u32[]{:S(2)}, u32[]{:S(2)}) collective-permute-start(f32[512,1024]{1,0:T(8,128)} %collective-permute-done.16.refs_3_), channel_id=1, source_target_pairs={{0,4},{4,0},{1,5},{5,1},{2,6},{6,2},{3,7},{7,3}} | collective-permute-start | bytes 6291464 | tf_op jit(solution)/shard_map/ppermute | solution.py:160
  1866.3 87.2 %collective-permute-start.15 = (f32[512,1024]{1,0:T(8,128)S(1)}, f32[512,1024]{1,0:T(8,128)}, u32[]{:S(2)}, u32[]{:S(2)}) collective-permute-start(f32[512,1024]{1,0:T(8,128)S(1)} %copy-done.3), channel_id=1, source_target_pairs={{0,4},{4,0},{1,5},{5,1},{2,6},{6,2},{3,7},{7,3}} | collective-permute-start | bytes 6291464 | tf_op jit(solution)/shard_map/ppermute | solution.py:160
  1911.6 143.5 %collective-permute-start.25 = (f32[512,1024]{1,0:T(8,128)S(1)}, f32[512,1024]{1,0:T(8,128)}, u32[]{:S(2)}, u32[]{:S(2)}) collective-permute-start(f32[512,1024]{1,0:T(8,128)S(1)} %collective-permute-done.21.refs_5_), channel_id=1, source_target_pairs={{0,1},{1,0},{2,3},{3,2},{4,5},{5,4},{6,7},{7,6}} | collective-permute-start | bytes 6291464 | tf_op jit(solution)/shard_map/ppermute | solution.py:160
  1911.8 143.3 %collective-permute-start.24 = (f32[512,1024]{1,0:T(8,128)}, f32[512,1024]{1,0:T(8,128)}, u32[]{:S(2)}, u32[]{:S(2)}) collective-permute-start(f32[512,1024]{1,0:T(8,128)} %collective-permute-done.19.refs_4_), channel_id=1, source_target_pairs={{0,1},{1,0},{2,3},{3,2},{4,5},{5,4},{6,7},{7,6}} | collective-permute-start | bytes 6291464 | tf_op jit(solution)/shard_map/ppermute | solution.py:160
  1953.4 101.7 %collective-permute-start.23 = (f32[512,1024]{1,0:T(8,128)}, f32[512,1024]{1,0:T(8,128)}, u32[]{:S(2)}, u32[]{:S(2)}) collective-permute-start(f32[512,1024]{1,0:T(8,128)} %collective-permute-done.17.refs_3_), channel_id=1, source_target_pairs={{0,1},{1,0},{2,3},{3,2},{4,5},{5,4},{6,7},{7,6}} | collective-permute-start | bytes 6291464 | tf_op jit(solution)/shard_map/ppermute | solution.py:160
  1953.4 101.7 %collective-permute-start.22 = (f32[512,1024]{1,0:T(8,128)}, f32[512,1024]{1,0:T(8,128)}, u32[]{:S(2)}, u32[]{:S(2)}) collective-permute-start(f32[512,1024]{1,0:T(8,128)} %collective-permute-done.15.refs_2_), channel_id=1, source_target_pairs={{0,1},{1,0},{2,3},{3,2},{4,5},{5,4},{6,7},{7,6}} | collective-permute-start | bytes 6291464 | tf_op jit(solution)/shard_map/ppermute | solution.py:160
  (24 other events, 1501.4 us)
Sparse Core Ops, SparseCore 0:
  16.1 19.1 all-gather.7
  110.2 23.5 all-gather.9
  135.3 18.2 all-gather.11
  323.1 27.0 all-gather.13
  874.8 27.8 all-gather.15
  904.1 28.4 all-gather.17
  934.8 23.3 reduce-scatter.6
  960.5 23.5 reduce-scatter.4
  985.7 28.6 all-gather.19
  1016.4 23.4 reduce-scatter.10
  1042.2 23.5 reduce-scatter.8
